TPU v7x, 32 devices: a whole 2x2x4 slice. The times are simulated.
32 devices in a mesh: wide: 16 (over z, x, core), narrow: 2 (over y).
Axes of the slice: x: 2, y: 2, z: 4, core: 2. Of those that a mesh axis runs over, the one named last changes fastest.
Arguments:
- diffusivity: float32 [64, 16, 256], P('wide', None, 'narrow'), may hold values from 0.06 to 0.13
- velocity: float32 [64, 16, 256], P('wide', None, 'narrow'), may hold values from 0 to 0.9
- damping: float32 [64, 16, 256], P('wide', None, 'narrow'), may hold values from 0.02 to 0.2
- input_amplitude: float32 [64, 64, 256], P(None, 'wide', 'narrow'), may hold values from -6 to 6
- output_amplitude: float32 [64, 64, 256], P(None, 'wide', 'narrow'), may hold values from -6 to 6
- input_height: int32 [64], replicated, may hold values from 0 to 15
- output_height: int32 [64], replicated, may hold values from 0 to 15
- start_block: float32 [64, 32], replicated, may hold values from -0.75 to 0.75
Outputs:
- direct_modes: float32 [32, 64, 16, 256], P(None, 'wide', None, 'narrow')
- adjoint_modes: float32 [32, 64, 16, 256], P(None, 'wide', None, 'narrow')
Inputs may be any that keep to these rules, and one draw needn't show every extreme that they name: Input j forces only the wall-parallel plane at wall-normal index input_height[j]. Output k weights only the wall-parallel plane at wall-normal index output_height[k].
All inputs are finite; a program needn't handle non-finite values.
Results may differ from a plain program's by a relative error of at most 0.0003.
Values sent between devices are 32-bit elements; how exact they have to be, the bound alone decides.
No kernel may reach another device: no remote copies, remote signals or barrier semaphores. Data moves between devices by JAX's collectives and lax.ppermute only.
A program may use at most 128 MiB of HBM per device.

v0:
```python
import functools
import math

import jax
import jax.numpy as jnp
from jax import lax
from jax.experimental import pallas as pl
from jax.experimental.pallas import tpu as pltpu
from jax.sharding import PartitionSpec as P

STEPS = 4
HIGH = lax.Precision.HIGHEST
LANES = 128
SUB = 8
SLOT = 32
PER = LANES // SLOT
LEFT = 0
RIGHT = 16
REACH = STEPS + SUB

VMEM = pl.BlockSpec(memory_space=pltpu.VMEM)
SMEM = pl.BlockSpec(memory_space=pltpu.SMEM)


def swaps(count):
    near = [(i, i ^ 1) for i in range(count) if i ^ 1 < count]
    far = [(i, ((i + 1) ^ 1) - 1) for i in range(count) if 0 <= ((i + 1) ^ 1) - 1 < count]
    return near, far


def lane_ids(shape):
    return lax.broadcasted_iota(jnp.int32, shape, len(shape) - 1)


def turn(value, amount):
    return pltpu.roll(value, amount % LANES, value.ndim - 1)


def edges(block, slot):
    within = lane_ids(block.shape) - slot * SLOT
    low = turn(block, slot * SLOT + LEFT + STEPS)
    high = turn(block, slot * SLOT + RIGHT - (LANES - SUB))
    is_low = (within >= LEFT + STEPS) & (within < LEFT + REACH)
    is_high = (within >= RIGHT) & (within < RIGHT + SUB)
    return jnp.where(is_low, low, jnp.where(is_high, high, 0.0))


def pack_kernel(
    inputs, width_x, depth_y, place_ref, rank_ref,
    amp_in, amp_out, diff, vel, damp, near, far,
    sorted_ref, cell_ref, rim_ref,
):
    own = width_x
    near_x = place_ref[0]
    far_x = place_ref[1]
    for system, source in ((0, amp_in), (1, amp_out)):
        base = system * inputs * width_x

        def move(j, carry, system=system, source=source, base=base):
            to = rank_ref[system, j]
            for x in range(width_x):
                sorted_ref[system, own + x, pl.ds(to, 1), :] = source[pl.ds(j * width_x + x, 1), :]
                row = base + j * width_x + x
                sorted_ref[system, near_x + x, pl.ds(to, 1), :] = near[pl.ds(row, 1), :]
                sorted_ref[system, far_x + x, pl.ds(to, 1), :] = far[pl.ds(row, 1), :]
            return carry

        lax.fori_loop(0, inputs, move, 0, unroll=4)
    start = 2 * inputs * width_x
    for which, source in enumerate((diff, vel, damp)):
        for x in range(width_x):
            rows = pl.ds(start + (which * width_x + x) * depth_y, depth_y)
            cell_ref[which, own + x] = source[x]
            cell_ref[which, near_x + x] = near[rows, :]
            cell_ref[which, far_x + x] = far[rows, :]
    groups = inputs // SUB
    rims = groups // PER
    extent = 3 * width_x
    tiles = depth_y // SUB

    def rim_row(x, carry):
        for system in range(2):
            for rim in range(rims):
                total = jnp.zeros((SUB, LANES), jnp.float32)
                for slot in range(PER):
                    group = rim * PER + slot
                    total = total + edges(sorted_ref[system, x, group * SUB : (group + 1) * SUB, :], slot)
                rim_ref[(system * rims + rim) * extent + x] = total
        pieces = [(which, tile) for which in range(3) for tile in range(tiles)]
        for at in range(0, len(pieces), PER):
            total = jnp.zeros((SUB, LANES), jnp.float32)
            for slot, (which, tile) in enumerate(pieces[at : at + PER]):
                total = total + edges(cell_ref[which, x, tile * SUB : (tile + 1) * SUB, :], slot)
            rim_ref[(2 * rims + at // PER) * extent + x] = total
        return carry

    lax.fori_loop(0, extent, rim_row, 0)


def split(value):
    first = value.astype(jnp.bfloat16)
    rest = value - first.astype(jnp.float32)
    second = rest.astype(jnp.bfloat16)
    third = (rest - second.astype(jnp.float32)).astype(jnp.bfloat16)
    return first, second, third


def window_kernel(
    inputs, width_x, depth_y, bounds_ref, flag_ref,
    sorted_ref, cell_ref, rim_ref, from_right, from_left, level_ref,
    direct_ref, adjoint_ref, gram_ref,
    amp, coef, ping, pong, field, total_ref,
):
    groups = inputs // SUB
    rims = groups // PER
    extent = 3 * width_x
    tiles = depth_y // SUB
    lanes = lane_ids((SUB, LANES))
    within = lanes % SLOT
    from_right_lane = (within >= RIGHT + SUB) & (within < RIGHT + REACH) & (flag_ref[0] > 0)
    from_left_lane = (within >= LEFT) & (within < LEFT + STEPS) & (flag_ref[1] > 0)

    def whole_rim(index):
        value = rim_ref[index]
        value = jnp.where(from_right_lane, turn(from_right[index], RIGHT + SUB - STEPS), value)
        return jnp.where(from_left_lane, turn(from_left[index], LEFT - RIGHT - STEPS), value)

    pieces = [(which, tile) for which in range(3) for tile in range(tiles)]

    def put(side, x, tile, diff, vel, damp):
        rows = slice(tile * SUB, (tile + 1) * SUB)
        coef[side, 0, x, rows, :] = 1.0 - 6.0 * diff - damp
        coef[side, 1, x, rows, :] = diff
        coef[side, 2, x, rows, :] = vel
        coef[side, 3, x, rows, :] = jnp.where(diff > 0.0, 1.0 / jnp.where(diff > 0.0, diff, 1.0), 0.0)

    def prepare(x, carry):
        for system in range(2):
            for rim in range(rims):
                amp[system, x, rim * SUB : (rim + 1) * SUB, :] = whole_rim((system * rims + rim) * extent + x)
        parts = {}
        for at in range(0, len(pieces), PER):
            packed = whole_rim((2 * rims + at // PER) * extent + x)
            for slot, piece in enumerate(pieces[at : at + PER]):
                alone = turn(jnp.where(lanes // SLOT == slot, packed, 0.0), -slot * SLOT)
                step = SLOT
                while step < LANES:
                    alone = alone + turn(alone, step)
                    step *= 2
                parts[piece] = alone
        for tile in range(tiles):
            rows = slice(tile * SUB, (tile + 1) * SUB)
            put(0, x, tile, *(cell_ref[which, x, rows, :] for which in range(3)))
            put(1, x, tile, *(parts[(which, tile)] for which in range(3)))
        return carry

    lax.fori_loop(0, extent, prepare, 0)

    def spread(side, which, x, y):
        return coef[side, which, x, pl.ds(y, SUB, stride=0), :]

    pad = 2

    def march(system, group, side, load_amp, levels_at):
        low0 = bounds_ref[system, group, 0]
        high0 = bounds_ref[system, group, 1]
        zero = jnp.zeros((SUB, LANES), jnp.float32)

        def blank(target, margin, low, high):
            for x in range(margin, extent - margin):
                for offset in (1, 2):
                    target[x, low - offset + pad] = zero
                    target[x, high + offset + pad] = zero

        heights = levels_at

        def begin(y, carry):
            here = heights == y
            for x in range(extent):
                value = jnp.where(here, load_amp(x), 0.0)
                if system:
                    value = value * spread(side, 1, x, y)
                ping[x, y + pad] = value
            return carry

        lax.fori_loop(low0, high0 + 1, begin, 0)
        blank(ping, 0, low0, high0)
        for level in range(1, STEPS + 1):
            source, target = (ping, pong) if level % 2 else (pong, ping)
            low = jnp.maximum(low0 - level, 0)
            high = jnp.minimum(high0 + level, depth_y - 1)

            def step(y, carry, level=level, source=source, target=target):
                rows = {}
                carried = {}
                for x in range(level - 1, extent - level + 1):
                    rows[x] = source[x, y + pad]
                    if system:
                        carried[x] = rows[x] * spread(side, 2, x, y)
                for x in range(level, extent - level):
                    here = rows[x]
                    behind, ahead = rows[x - 1], rows[x + 1]
                    beside = (source[x, y + pad - 1] + source[x, y + pad + 1]) + (turn(here, 1) + turn(here, -1))
                    if system:
                        drift = carried[x + 1] - carried[x - 1]
                    else:
                        drift = spread(side, 2, x, y) * (behind - ahead)
                    total = beside + (behind + ahead) + drift
                    if system and level == STEPS:
                        value = spread(side, 0, x, y) * (here * spread(side, 3, x, y)) + total
                    else:
                        value = spread(side, 0, x, y) * here + spread(side, 1, x, y) * total
                    if level == STEPS:
                        field[system, x - level, y, group] = value
                    else:
                        target[x, y + pad] = value
                return carry

            lax.fori_loop(low, high + 1, step, 0)
            if level < STEPS:
                blank(target, level, low, high)
            else:

                def clear(y, carry):
                    for x in range(width_x):
                        field[system, x, y, group] = zero
                    return carry

                lax.fori_loop(0, low, clear, 0)
                lax.fori_loop(high + 1, depth_y, clear, 0)

    def main_group(group, carry):
        at = pl.multiple_of(group * SUB, SUB)
        for system in range(2):
            march(
                system, group, 0,
                lambda x, system=system: sorted_ref[system, x, pl.ds(at, SUB), :],
                level_ref[system, pl.ds(at, SUB), :],
            )
        return carry

    lax.fori_loop(0, groups, main_group, 0)

    def rim_group(rim, carry):
        at = pl.multiple_of(rim * SUB, SUB)
        for system in range(2):
            march(
                system, groups + rim, 1,
                lambda x, system=system: amp[system, x, pl.ds(at, SUB), :],
                level_ref[system, pl.ds(inputs + at, SUB), :],
            )
        return carry

    lax.fori_loop(0, rims, rim_group, 0)

    total_ref[...] = jnp.zeros_like(total_ref)
    pairs = depth_y // 2

    def fold(pair, carry):
        x = pair // pairs
        y = (pair % pairs) * 2
        stacked = []
        for system in range(2):
            halves = []
            for half in range(2):
                merged = []
                for group in range(groups):
                    edge = field[system, x, y + half, groups + group // PER]
                    slot = group % PER
                    value = field[system, x, y + half, group]
                    low = turn(edge, -(slot * SLOT + LEFT + STEPS))
                    high = turn(edge, LANES - STEPS - (slot * SLOT + RIGHT + STEPS))
                    value = jnp.where(lanes < STEPS, low, jnp.where(lanes >= LANES - STEPS, high, value))
                    merged.append(value)
                halves.append(jnp.concatenate(merged, axis=0))
            whole = jnp.concatenate(halves, axis=1)
            first, second, third = split(whole)
            out = adjoint_ref if system else direct_ref
            out[pair, 0:inputs, :] = first
            out[pair, inputs : 2 * inputs, :] = second
            stacked.append(jnp.concatenate([first, second, third], axis=0))
        total_ref[...] += lax.dot_general(
            stacked[1], stacked[0], (((1,), (1,)), ((), ())), preferred_element_type=jnp.float32
        )
        return carry

    lax.fori_loop(0, width_x * pairs, fold, 0)

    def part(row, column):
        return total_ref[row * inputs : (row + 1) * inputs, column * inputs : (column + 1) * inputs]

    gram_ref[...] = (
        (part(0, 2) + part(2, 0)) + part(1, 1) + (part(0, 1) + part(1, 0)) + part(0, 0)
    )


def eliminate(matrix):
    size = matrix.shape[0]
    row_ids = lax.broadcasted_iota(jnp.int32, (size, 2 * size), 0)
    column_ids = lax.broadcasted_iota(jnp.int32, (size, 2 * size), 1)
    unit = jnp.where(column_ids - size == row_ids, 1.0, 0.0)
    work = jnp.where(column_ids < size, jnp.concatenate([matrix, matrix], axis=1), unit)
    pivots = jnp.ones((size, 1), jnp.float32)
    ids = lax.broadcasted_iota(jnp.int32, (size, 1), 0)
    for k in range(size):
        row = work[k : k + 1, :]
        pivot = work[k : k + 1, k : k + 1]
        pivots = jnp.where(ids == k, pivot, pivots)
        factor = jnp.where(ids > k, work[:, k : k + 1] / pivot, 0.0)
        work = work - factor * row
    return work[:, size:], pivots


def product(left, right, contract):
    return lax.dot_general(
        left, right, (contract, ((), ())), precision=HIGH, preferred_element_type=jnp.float32
    )


def modes_kernel(
    inputs, width_x, depth_y, scale, rank_ref,
    gram_ref, start_ref, direct_ref, adjoint_ref,
    direct_out, adjoint_out,
    start_sorted,
):
    modes = start_ref.shape[1]

    def move(j, carry):
        start_sorted[pl.ds(rank_ref[0, j], 1), :] = start_ref[pl.ds(j, 1), :]
        return carry

    lax.fori_loop(0, inputs, move, 0, unroll=8)
    gram = gram_ref[...] * scale

    def orthonormal(block):
        lower, pivots = eliminate(product(block, block, ((0,), (0,))))
        return product(block, lower * lax.rsqrt(pivots), ((1,), (1,)))

    first = orthonormal(product(gram, start_sorted[...], ((1,), (0,))))
    right = orthonormal(product(gram, first, ((0,), (0,))))
    reached = product(gram, right, ((1,), (0,)))
    lower, pivots = eliminate(product(reached, reached, ((0,), (0,))))
    root = jnp.sqrt(pivots)
    quarter = jnp.sqrt(root)
    mixes = (
        product(lower / quarter, right, ((1,), (1,))),
        product(lower / (root * quarter), reached, ((1,), (1,))),
    )
    pairs = depth_y // 2
    for mix, source, out in zip(mixes, (direct_ref, adjoint_ref), (direct_out, adjoint_out)):
        high, low, rest = split(mix)
        stacked = jnp.concatenate(
            [jnp.concatenate([high, high], axis=1), jnp.concatenate([low, low], axis=1)], axis=0
        )

        def project(pair, carry, stacked=stacked, source=source, out=out):
            both = jnp.dot(stacked, source[pair], preferred_element_type=jnp.float32)
            value = both[:modes] + both[modes:]
            for half in range(2):
                out[pl.ds(pair * 2 + half, modes, stride=width_x * depth_y), :] = value[
                    :, half * LANES : (half + 1) * LANES
                ]
            return carry

        lax.fori_loop(0, width_x * pairs, project, 0, unroll=4)


def ordering(height):
    count = height.shape[0]
    at = lax.iota(jnp.int32, count)
    ahead = (height[None, :] < height[:, None]) | (
        (height[None, :] == height[:, None]) & (at[None, :] < at[:, None])
    )
    rank = jnp.sum(ahead.astype(jnp.int32), axis=1)
    ordered = jnp.sum(jnp.where(rank[None, :] == at[:, None], height[None, :], 0), axis=1)
    return rank, ordered


def on_device(
    diffusivity,
    velocity,
    damping,
    input_amplitude,
    output_amplitude,
    input_height,
    output_height,
    start_block,
):
    inputs, width_x, width_z = input_amplitude.shape
    depth_y = diffusivity.shape[1]
    rank_count = start_block.shape[1]
    wide = lax.axis_size("wide")
    narrow = lax.axis_size("narrow")
    assert width_z == LANES and width_x == STEPS and inputs % (SUB * PER) == 0
    f32 = jnp.float32
    extent = 3 * width_x
    groups = inputs // SUB
    rims = groups // PER
    tiles = depth_y // SUB

    flat_in = input_amplitude.reshape(-1, width_z)
    flat_out = output_amplitude.reshape(-1, width_z)
    sent = jnp.concatenate(
        [flat_in, flat_out]
        + [cell.reshape(-1, width_z) for cell in (diffusivity, velocity, damping)]
    )
    near_pairs, far_pairs = swaps(wide)
    near = lax.ppermute(sent, "wide", near_pairs)
    far = lax.ppermute(sent, "wide", far_pairs)

    orders = [ordering(height) for height in (input_height, output_height)]
    ranks = jnp.stack([rank for rank, ordered in orders])
    heights = jnp.stack([ordered for rank, ordered in orders])
    by_group = heights.reshape(2, groups, SUB)
    by_rim = heights.reshape(2, rims, PER * SUB)
    bounds = jnp.concatenate(
        [
            jnp.stack([by_group[:, :, 0], by_group[:, :, -1]], axis=-1),
            jnp.stack([by_rim[:, :, 0], by_rim[:, :, -1]], axis=-1),
        ],
        axis=1,
    )
    rim_levels = heights.reshape(2, rims, PER, SUB).transpose(0, 1, 3, 2)
    levels = jnp.concatenate(
        [
            jnp.broadcast_to(heights[:, :, None], (2, inputs, LANES)),
            jnp.repeat(rim_levels, SLOT, axis=-1).reshape(2, rims * SUB, LANES),
        ],
        axis=1,
    )

    odd = lax.axis_index("wide") % 2
    place = jnp.stack([2 * width_x * (1 - odd), 2 * width_x * odd])
    rim_count = (2 * rims + -(-3 * tiles // PER)) * extent
    arranged, cells, rim = pl.pallas_call(
        functools.partial(pack_kernel, inputs, width_x, depth_y),
        out_shape=(
            jax.ShapeDtypeStruct((2, extent, inputs, LANES), f32),
            jax.ShapeDtypeStruct((3, extent, depth_y, LANES), f32),
            jax.ShapeDtypeStruct((rim_count, SUB, LANES), f32),
        ),
        in_specs=[SMEM, SMEM] + [VMEM] * 7,
        out_specs=(VMEM, VMEM, VMEM),
        name="pack",
    )(place, ranks, flat_in, flat_out, diffusivity, velocity, damping, near, far)

    if narrow == 2:
        from_right = lax.ppermute(rim, "narrow", [(0, 1), (1, 0)])
        from_left = from_right
    else:
        from_right = lax.ppermute(rim, "narrow", [(i + 1, i) for i in range(narrow - 1)])
        from_left = lax.ppermute(rim, "narrow", [(i, i + 1) for i in range(narrow - 1)])
    side = lax.axis_index("narrow")
    flags = jnp.stack([(side + 1 < narrow).astype(jnp.int32), (side > 0).astype(jnp.int32)])

    pair_count = width_x * depth_y // 2
    direct, adjoint, gram = pl.pallas_call(
        functools.partial(window_kernel, inputs, width_x, depth_y),
        out_shape=(
            jax.ShapeDtypeStruct((pair_count, 2 * inputs, 2 * LANES), jnp.bfloat16),
            jax.ShapeDtypeStruct((pair_count, 2 * inputs, 2 * LANES), jnp.bfloat16),
            jax.ShapeDtypeStruct((inputs, inputs), f32),
        ),
        in_specs=[SMEM, SMEM] + [VMEM] * 6,
        out_specs=(VMEM, VMEM, VMEM),
        scratch_shapes=[
            pltpu.VMEM((2, extent, rims * SUB, LANES), f32),
            pltpu.VMEM((2, 4, extent, depth_y, LANES), f32),
            pltpu.VMEM((extent, depth_y + 4, SUB, LANES), f32),
            pltpu.VMEM((extent, depth_y + 4, SUB, LANES), f32),
            pltpu.VMEM((2, width_x, depth_y, groups + rims, SUB, LANES), f32),
            pltpu.VMEM((3 * inputs, 3 * inputs), f32),
        ],
        name="window",
    )(bounds, flags, arranged, cells, rim, from_right, from_left, levels)

    step = 1
    while step < wide:
        gram = gram + lax.ppermute(gram, "wide", [(i, i ^ step) for i in range(wide)])
        step *= 2
    step = 1
    while step < narrow:
        gram = gram + lax.ppermute(gram, "narrow", [(i, i ^ step) for i in range(narrow)])
        step *= 2

    scale = 1.0 / math.sqrt(width_x * wide * depth_y * width_z * narrow)
    shape = jax.ShapeDtypeStruct((rank_count * width_x * depth_y, LANES), f32)
    direct_modes, adjoint_modes = pl.pallas_call(
        functools.partial(modes_kernel, inputs, width_x, depth_y, scale),
        out_shape=(shape, shape),
        in_specs=[SMEM] + [VMEM] * 4,
        out_specs=(VMEM, VMEM),
        scratch_shapes=[pltpu.VMEM((inputs, rank_count), f32)],
        name="modes",
    )(ranks, gram, start_block, direct, adjoint)
    full = (rank_count, width_x, depth_y, width_z)
    return (direct_modes.reshape(full), adjoint_modes.reshape(full))


def solution(mesh):
    in_specs = (
        P("wide", None, "narrow"),
        P("wide", None, "narrow"),
        P("wide", None, "narrow"),
        P(None, "wide", "narrow"),
        P(None, "wide", "narrow"),
        P(),
        P(),
        P(),
    )
    out_specs = (P(None, "wide", None, "narrow"), P(None, "wide", None, "narrow"))
    return jax.shard_map(
        on_device, mesh=mesh, in_specs=in_specs, out_specs=out_specs, check_vma=False
    )
```

profile of v0, /device:TPU:0, one launch (start us, length us, event | category | flops | bytes accessed | tf_op | source)
XLA Modules:
  0.0 143.0 jit_solution(16209117667308007596)
XLA Ops:
  0.6 0.9 constant_dynamic-update-slice_fusion.8
  1.5 0.9 constant_dynamic-update-slice_fusion.7
  2.5 0.8 constant_dynamic-update-slice_fusion.6
  3.2 0.8 constant_dynamic-update-slice_fusion.5
  4.0 0.8 constant_dynamic-update-slice_fusion.4
  4.8 0.8 collective-permute-start.1
  5.6 4.4 %collective-permute-start = (f32[704,128]{1,0:T(8,128)S(1)}, f32[704,128]{1,0:T(8,128)S(1)}, u32[]{:S(2)}, u32[]{:S(2)}) collective-permute-start(f32[704,128]{1,0:T(8,128)S(1)} %constant_dynamic-update-slice_fusion.4), channel_id=1, source_target_pairs={{0,2},{2,0},{4,6},{6,4},{8,10},{10,8},{12,14},{14,12},{16,18},{18,... | collective-permute-start | bytes 1081352 | tf_op jit(solution)/shard_map/ppermute | solution.py:408
  9.9 0.9 convert_reduce_fusion
  10.9 0.8 select_reduce_fusion
  11.6 0.1 stack.72
  11.7 0.1 stack.86
  11.8 0.9 convert_reduce_fusion.1
  12.7 0.8 select_reduce_fusion.1
  13.5 0.1 stack.71
  13.6 0.1 stack.85
  13.7 0.1 stack.67
  13.8 0.1 fusion.5
  13.8 0.5 pad_add_fusion.1.rank_ref
  14.4 0.6 pad_add_fusion.3.place_ref
  14.9 0.1 stack.68
  15.0 0.1 copy.23
  15.1 0.1 broadcast_in_dim.20
  15.2 0.1 reshape_reshape.3
  15.3 0.1 fusion.4
  15.4 0.7 copy-done.1
  16.2 0.7 copy-done.2
  16.9 4.6 %pack.1 = (f32[2,12,64,128]{3,2,1,0:T(8,128)}, f32[3,12,16,128]{3,2,1,0:T(8,128)}, f32[72,8,128]{2,1,0:T(8,128)}) custom-call(s32[2]{0:T(128)} %pad_add_fusion.3.place_ref, s32[2,64]{1,0:T(2,128)} %pad_add_fusion.1.rank_ref, f32[256,128]{1,0:T(8,128)} %bitcast.18, f32[256,128]{1,0:T(8,128)} %bitcast.20, f32[4,16,128]{2,1,0:T(8,128)} %diff.1, ...), custom_call_target="tpu_custom_call" | custom-call | tf_op jit(solution)/shard_map/pack/pallas_call | solution.py:435
  21.5 1.5 %collective-permute-start.2 = (f32[72,8,128]{2,1,0:T(8,128)}, f32[72,8,128]{2,1,0:T(8,128)S(1)}, u32[]{:S(2)}, u32[]{:S(2)}) collective-permute-start(f32[72,8,128]{2,1,0:T(8,128)} %get-tuple-element.12.rim_ref), channel_id=1, source_target_pairs={{0,1},{1,0},{2,3},{3,2},{4,5},{5,4},{6,7},{7,6},{8,9},{9,8},{10,11... | collective-permute-start | bytes 884744 | tf_op jit(solution)/shard_map/ppermute | solution.py:448
  23.0 0.6 add_convert_fusion.flag_ref
  23.6 0.7 add_add_fusion.bounds_ref
  24.3 0.6 pad_add_fusion.level_ref
  25.0 4.9 %collective-permute-done.2.from_right.from_left = f32[72,8,128]{2,1,0:T(8,128)S(1)} collective-permute-done((f32[72,8,128]{2,1,0:T(8,128)}, f32[72,8,128]{2,1,0:T(8,128)S(1)}, u32[]{:S(2)}, u32[]{:S(2)}) %collective-permute-start.2) | collective-permute-done | bytes 294944 | tf_op jit(solution)/shard_map/ppermute | solution.py:448
  29.9 0.7 copy-done
  30.6 74.2 %window.1 = (bf16[32,128,256]{2,1,0:T(8,128)(2,1)}, bf16[32,128,256]{2,1,0:T(8,128)(2,1)}, f32[64,64]{1,0:T(8,128)}) custom-call(s32[2,10,2]{2,1,0:T(8,128)} %add_add_fusion.bounds_ref, s32[2]{0:T(128)} %add_convert_fusion.flag_ref, f32[2,12,64,128]{3,2,1,0:T(8,128)} %get-tuple-element.10.sorted_ref, f32[3,12,16,128]{3,2,1,0:T(8,128)} %get-tuple-element.11.cell_ref, ...), custom_call_target="tpu_custom_call" | custom-call | tf_op jit(solution)/shard_map/window/pallas_call | solution.py:457
  104.8 1.5 %collective-permute-start.3 = (f32[64,64]{1,0:T(8,128)}, f32[64,64]{1,0:T(8,128)S(1)}, u32[]{:S(2)}, u32[]{:S(2)}) collective-permute-start(f32[64,64]{1,0:T(8,128)} %get-tuple-element.13), channel_id=1, source_target_pairs={{0,2},{2,0},{4,6},{6,4},{8,10},{10,8},{12,14},{14,12},{16,18},{18,... | collective-permute-start | bytes 49160 | tf_op jit(solution)/shard_map/ppermute | solution.py:479
  106.3 1.1 collective-permute-done.3
  107.4 0.8 add.24
  108.1 2.4 %collective-permute-start.4 = (f32[64,64]{1,0:T(8,128)S(1)}, f32[64,64]{1,0:T(8,128)S(1)}, u32[]{:S(2)}, u32[]{:S(2)}) collective-permute-start(f32[64,64]{1,0:T(8,128)S(1)} %add.24), channel_id=1, source_target_pairs={{0,4},{2,6},{4,0},{6,2},{8,12},{10,14},{12,8},{14,10},{16,20},{18,... | collective-permute-start | bytes 49160 | tf_op jit(solution)/shard_map/ppermute | solution.py:479
  110.5 1.9 %collective-permute-done.4 = f32[64,64]{1,0:T(8,128)S(1)} collective-permute-done((f32[64,64]{1,0:T(8,128)S(1)}, f32[64,64]{1,0:T(8,128)S(1)}, u32[]{:S(2)}, u32[]{:S(2)}) %collective-permute-start.4) | collective-permute-done | bytes 16416 | tf_op jit(solution)/shard_map/ppermute | solution.py:479
  112.4 1.9 %collective-permute-start.5 = (f32[64,64]{1,0:T(8,128)S(1)}, f32[64,64]{1,0:T(8,128)S(1)}, u32[]{:S(2)}, u32[]{:S(2)}) collective-permute-start(f32[64,64]{1,0:T(8,128)S(1)} %add.25), channel_id=1, source_target_pairs={{0,8},{2,10},{4,12},{6,14},{8,0},{10,2},{12,4},{14,6},{16,24},{18,... | collective-permute-start | bytes 49160 | tf_op jit(solution)/shard_map/ppermute | solution.py:479
  114.3 2.0 %collective-permute-done.5 = f32[64,64]{1,0:T(8,128)S(1)} collective-permute-done((f32[64,64]{1,0:T(8,128)S(1)}, f32[64,64]{1,0:T(8,128)S(1)}, u32[]{:S(2)}, u32[]{:S(2)}) %collective-permute-start.5) | collective-permute-done | bytes 16416 | tf_op jit(solution)/shard_map/ppermute | solution.py:479
  116.4 2.9 %collective-permute-start.6 = (f32[64,64]{1,0:T(8,128)S(1)}, f32[64,64]{1,0:T(8,128)S(1)}, u32[]{:S(2)}, u32[]{:S(2)}) collective-permute-start(f32[64,64]{1,0:T(8,128)S(1)} %add.26), channel_id=1, source_target_pairs={{0,16},{2,18},{4,20},{6,22},{8,24},{10,26},{12,28},{14,30},{16,0},... | collective-permute-start | bytes 49160 | tf_op jit(solution)/shard_map/ppermute | solution.py:479
  119.2 1.9 %collective-permute-done.6 = f32[64,64]{1,0:T(8,128)S(1)} collective-permute-done((f32[64,64]{1,0:T(8,128)S(1)}, f32[64,64]{1,0:T(8,128)S(1)}, u32[]{:S(2)}, u32[]{:S(2)}) %collective-permute-start.6) | collective-permute-done | bytes 16416 | tf_op jit(solution)/shard_map/ppermute | solution.py:479
  121.2 1.5 %collective-permute-start.7 = (f32[64,64]{1,0:T(8,128)S(1)}, f32[64,64]{1,0:T(8,128)S(1)}, u32[]{:S(2)}, u32[]{:S(2)}) collective-permute-start(f32[64,64]{1,0:T(8,128)S(1)} %add.27), channel_id=1, source_target_pairs={{0,1},{1,0},{2,3},{3,2},{4,5},{5,4},{6,7},{7,6},{8,9},{9,8},{10,11... | collective-permute-start | bytes 49160 | tf_op jit(solution)/shard_map/ppermute | solution.py:483
  122.7 0.7 copy.24.start_ref
  123.4 1.7 %collective-permute-done.7 = f32[64,64]{1,0:T(8,128)S(1)} collective-permute-done((f32[64,64]{1,0:T(8,128)S(1)}, f32[64,64]{1,0:T(8,128)S(1)}, u32[]{:S(2)}, u32[]{:S(2)}) %collective-permute-start.7) | collective-permute-done | bytes 16416 | tf_op jit(solution)/shard_map/ppermute | solution.py:483
  125.1 0.6 add.28.gram_ref
  125.7 17.3 %modes.1 = (f32[2048,128]{1,0:T(8,128)}, f32[2048,128]{1,0:T(8,128)}) custom-call(s32[2,64]{1,0:T(2,128)} %pad_add_fusion.1.rank_ref, f32[64,64]{1,0:T(8,128)} %add.28.gram_ref, f32[64,32]{1,0:T(8,128)} %copy.24.start_ref, bf16[32,128,256]{2,1,0:T(8,128)(2,1)} %get-tuple-element.14.direct_ref, bf16[32,128,256]{2,1,0:T(8,128)(2,1)} %get-tuple-element.15.adjoint_ref), custom_call_target="tpu_custom_call" | custom-call | tf_op jit(solution)/shard_map/modes/pallas_call | solution.py:488
  (17 shorter events, 0.1 us)
Async XLA Ops:
  4.8 117.9 %copy-start.3 = (f32[64,32]{0,1:T(8,128)S(1)}, f32[64,32]{0,1:T(8,128)}, u32[]{:S(2)}) copy-start(f32[64,32]{0,1:T(8,128)} %param.15) | copy-start | bytes 24580
  4.8 10.7 %collective-permute-start.1 = (f32[704,128]{1,0:T(8,128)S(1)}, f32[704,128]{1,0:T(8,128)S(1)}, u32[]{:S(2)}, u32[]{:S(2)}) collective-permute-start(f32[704,128]{1,0:T(8,128)S(1)} %constant_dynamic-update-slice_fusion.4), channel_id=1, source_target_pairs={{2,4},{4,2},{6,8},{8,6},{10,12},{12,10},{14,16},{16,14},{18,20},{2... | collective-permute-start | bytes 1081352 | tf_op jit(solution)/shard_map/ppermute | solution.py:409
  5.6 9.8 %collective-permute-start = (f32[704,128]{1,0:T(8,128)S(1)}, f32[704,128]{1,0:T(8,128)S(1)}, u32[]{:S(2)}, u32[]{:S(2)}) collective-permute-start(f32[704,128]{1,0:T(8,128)S(1)} %constant_dynamic-update-slice_fusion.4), channel_id=1, source_target_pairs={{0,2},{2,0},{4,6},{6,4},{8,10},{10,8},{12,14},{14,12},{16,18},{18,... | collective-permute-start | bytes 1081352 | tf_op jit(solution)/shard_map/ppermute | solution.py:408
  15.4 0.7 copy-start.1
  16.2 0.7 copy-start.2
  21.5 8.4 %collective-permute-start.2 = (f32[72,8,128]{2,1,0:T(8,128)}, f32[72,8,128]{2,1,0:T(8,128)S(1)}, u32[]{:S(2)}, u32[]{:S(2)}) collective-permute-start(f32[72,8,128]{2,1,0:T(8,128)} %get-tuple-element.12.rim_ref), channel_id=1, source_target_pairs={{0,1},{1,0},{2,3},{3,2},{4,5},{5,4},{6,7},{7,6},{8,9},{9,8},{10,11... | collective-permute-start | bytes 884744 | tf_op jit(solution)/shard_map/ppermute | solution.py:448
  29.9 0.7 copy-start
  104.8 2.6 %collective-permute-start.3 = (f32[64,64]{1,0:T(8,128)}, f32[64,64]{1,0:T(8,128)S(1)}, u32[]{:S(2)}, u32[]{:S(2)}) collective-permute-start(f32[64,64]{1,0:T(8,128)} %get-tuple-element.13), channel_id=1, source_target_pairs={{0,2},{2,0},{4,6},{6,4},{8,10},{10,8},{12,14},{14,12},{16,18},{18,... | collective-permute-start | bytes 49160 | tf_op jit(solution)/shard_map/ppermute | solution.py:479
  108.1 4.3 %collective-permute-start.4 = (f32[64,64]{1,0:T(8,128)S(1)}, f32[64,64]{1,0:T(8,128)S(1)}, u32[]{:S(2)}, u32[]{:S(2)}) collective-permute-start(f32[64,64]{1,0:T(8,128)S(1)} %add.24), channel_id=1, source_target_pairs={{0,4},{2,6},{4,0},{6,2},{8,12},{10,14},{12,8},{14,10},{16,20},{18,... | collective-permute-start | bytes 49160 | tf_op jit(solution)/shard_map/ppermute | solution.py:479
  112.4 3.9 %collective-permute-start.5 = (f32[64,64]{1,0:T(8,128)S(1)}, f32[64,64]{1,0:T(8,128)S(1)}, u32[]{:S(2)}, u32[]{:S(2)}) collective-permute-start(f32[64,64]{1,0:T(8,128)S(1)} %add.25), channel_id=1, source_target_pairs={{0,8},{2,10},{4,12},{6,14},{8,0},{10,2},{12,4},{14,6},{16,24},{18,... | collective-permute-start | bytes 49160 | tf_op jit(solution)/shard_map/ppermute | solution.py:479
  116.4 4.8 %collective-permute-start.6 = (f32[64,64]{1,0:T(8,128)S(1)}, f32[64,64]{1,0:T(8,128)S(1)}, u32[]{:S(2)}, u32[]{:S(2)}) collective-permute-start(f32[64,64]{1,0:T(8,128)S(1)} %add.26), channel_id=1, source_target_pairs={{0,16},{2,18},{4,20},{6,22},{8,24},{10,26},{12,28},{14,30},{16,0},... | collective-permute-start | bytes 49160 | tf_op jit(solution)/shard_map/ppermute | solution.py:479
  121.2 3.9 %collective-permute-start.7 = (f32[64,64]{1,0:T(8,128)S(1)}, f32[64,64]{1,0:T(8,128)S(1)}, u32[]{:S(2)}, u32[]{:S(2)}) collective-permute-start(f32[64,64]{1,0:T(8,128)S(1)} %add.27), channel_id=1, source_target_pairs={{0,1},{1,0},{2,3},{3,2},{4,5},{5,4},{6,7},{7,6},{8,9},{9,8},{10,11... | collective-permute-start | bytes 49160 | tf_op jit(solution)/shard_map/ppermute | solution.py:483
where the time goes:
time: 143 us
  Pallas kernels  96.1 us (67%)
  starting transfers between devices  16.9 us (12%)
  waiting for transfers between devices  13.5 us (9%)
  local copies, waits for them, and re-layouts  8 us (6%)
  other arithmetic  7.75 us (5%)
    pallas_call x1, Pallas kernels, on_device(): pl.pallas_call(functools.partial(window_kernel, inputs, width_x, depth_y)...  74.2 us
    pallas_call x1, Pallas kernels, on_device(): pl.pallas_call(functools.partial(modes_kernel, inputs, width_x, depth_y,...  17.3 us
    ppermute x4, starting transfers between devices, on_device(): lax.ppermute(gram, 'wide', [(i, i ^ step) for i in range(wide)])  8.69 us
    ppermute x4, waiting for transfers between devices, on_device(): lax.ppermute(gram, 'wide', [(i, i ^ step) for i in range(wide)])  6.92 us
    unnamed x15, local copies, waits for them, and re-layouts  6.23 us
    ppermute x1, waiting for transfers between devices, on_device(): from_right = lax.ppermute(rim, 'narrow', [(0, 1), (1, 0)])  4.91 us
    pallas_call x1, Pallas kernels, on_device(): pl.pallas_call(functools.partial(pack_kernel, inputs, width_x, depth_y),...  4.61 us
    ppermute x1, starting transfers between devices, on_device(): near = lax.ppermute(sent, 'wide', near_pairs)  4.37 us
  transfers between devices with their start and end apart: 8, of which 6 were waited for; matrix products, arithmetic and copies ran while one was open for 6% of the time, Pallas kernels for 0%

commit v1 on v0

--- a/solution.py
+++ b/solution.py
@@ -45,32 +45,45 @@
     return jnp.where(is_low, low, jnp.where(is_high, high, 0.0))
 
 
+def stage_kernel(*refs):
+    sources, target, sems = refs[:-2], refs[-2], refs[-1]
+    copies = []
+    at = 0
+    for index, source in enumerate(sources):
+        count = source.shape[0]
+        copies.append(pltpu.make_async_copy(source, target.at[pl.ds(at, count)], sems.at[index]))
+        at += count
+    for copy in copies:
+        copy.start()
+    for copy in copies:
+        copy.wait()
+
+
 def pack_kernel(
-    inputs, width_x, depth_y, place_ref, rank_ref,
-    amp_in, amp_out, diff, vel, damp, near, far,
+    inputs, width_x, depth_y, place_ref, rank_ref, here, near, far,
     sorted_ref, cell_ref, rim_ref,
 ):
     own = width_x
     near_x = place_ref[0]
     far_x = place_ref[1]
-    for system, source in ((0, amp_in), (1, amp_out)):
+    for system in range(2):
         base = system * inputs * width_x
 
-        def move(j, carry, system=system, source=source, base=base):
+        def move(j, carry, system=system, base=base):
             to = rank_ref[system, j]
             for x in range(width_x):
-                sorted_ref[system, own + x, pl.ds(to, 1), :] = source[pl.ds(j * width_x + x, 1), :]
                 row = base + j * width_x + x
+                sorted_ref[system, own + x, pl.ds(to, 1), :] = here[pl.ds(row, 1), :]
                 sorted_ref[system, near_x + x, pl.ds(to, 1), :] = near[pl.ds(row, 1), :]
                 sorted_ref[system, far_x + x, pl.ds(to, 1), :] = far[pl.ds(row, 1), :]
             return carry
 
         lax.fori_loop(0, inputs, move, 0, unroll=4)
     start = 2 * inputs * width_x
-    for which, source in enumerate((diff, vel, damp)):
+    for which in range(3):
         for x in range(width_x):
             rows = pl.ds(start + (which * width_x + x) * depth_y, depth_y)
-            cell_ref[which, own + x] = source[x]
+            cell_ref[which, own + x] = here[rows, :]
             cell_ref[which, near_x + x] = near[rows, :]
             cell_ref[which, far_x + x] = far[rows, :]
     groups = inputs // SUB
@@ -94,7 +107,7 @@
             rim_ref[(2 * rims + at // PER) * extent + x] = total
         return carry
 
-    lax.fori_loop(0, extent, rim_row, 0)
+    lax.fori_loop(0, extent, rim_row, 0, unroll=extent)
 
 
 def split(value):
@@ -128,11 +141,10 @@
     pieces = [(which, tile) for which in range(3) for tile in range(tiles)]
 
     def put(side, x, tile, diff, vel, damp):
-        rows = slice(tile * SUB, (tile + 1) * SUB)
-        coef[side, 0, x, rows, :] = 1.0 - 6.0 * diff - damp
-        coef[side, 1, x, rows, :] = diff
-        coef[side, 2, x, rows, :] = vel
-        coef[side, 3, x, rows, :] = jnp.where(diff > 0.0, 1.0 / jnp.where(diff > 0.0, diff, 1.0), 0.0)
+        inverse = jnp.where(diff > 0.0, 1.0 / jnp.where(diff > 0.0, diff, 1.0), 0.0)
+        for which, value in enumerate((1.0 - 6.0 * diff - damp, diff, vel, inverse)):
+            for y in range(SUB):
+                coef[side, which, x, tile * SUB + y] = jnp.broadcast_to(value[y : y + 1, :], (SUB, LANES))
 
     def prepare(x, carry):
         for system in range(2):
@@ -154,104 +166,105 @@
             put(1, x, tile, *(parts[(which, tile)] for which in range(3)))
         return carry
 
-    lax.fori_loop(0, extent, prepare, 0)
+    lax.fori_loop(0, extent, prepare, 0, unroll=extent)
 
     def spread(side, which, x, y):
-        return coef[side, which, x, pl.ds(y, SUB, stride=0), :]
+        return coef[side, which, x, y]
 
     pad = 2
-
-    def march(system, group, side, load_amp, levels_at):
-        low0 = bounds_ref[system, group, 0]
-        high0 = bounds_ref[system, group, 1]
-        zero = jnp.zeros((SUB, LANES), jnp.float32)
-
-        def blank(target, margin, low, high):
+    zero = jnp.zeros((SUB, LANES), jnp.float32)
+
+    def march(system):
+        units = range(groups + rims)
+        side = [int(unit >= groups) for unit in units]
+        low0 = [bounds_ref[system, unit, 0] for unit in units]
+        high0 = [bounds_ref[system, unit, 1] for unit in units]
+
+        def blank(target, unit, margin, low, high):
             for x in range(margin, extent - margin):
                 for offset in (1, 2):
-                    target[x, low - offset + pad] = zero
-                    target[x, high + offset + pad] = zero
-
-        heights = levels_at
-
-        def begin(y, carry):
-            here = heights == y
-            for x in range(extent):
-                value = jnp.where(here, load_amp(x), 0.0)
-                if system:
-                    value = value * spread(side, 1, x, y)
-                ping[x, y + pad] = value
-            return carry
-
-        lax.fori_loop(low0, high0 + 1, begin, 0)
-        blank(ping, 0, low0, high0)
+                    target[unit, x, low - offset + pad] = zero
+                    target[unit, x, high + offset + pad] = zero
+
+        for unit in units:
+            rows = slice(unit * SUB, (unit + 1) * SUB)
+            heights = level_ref[system, rows, :]
+
+            def begin(y, carry, unit=unit, rows=rows, heights=heights):
+                here = heights == y
+                for x in range(extent):
+                    if side[unit]:
+                        value = amp[system, x, (unit - groups) * SUB : (unit - groups + 1) * SUB, :]
+                    else:
+                        value = sorted_ref[system, x, rows, :]
+                    value = jnp.where(here, value, 0.0)
+                    if system:
+                        value = value * spread(side[unit], 1, x, y)
+                    ping[unit, x, y + pad] = value
+                return carry
+
+            lax.fori_loop(low0[unit], high0[unit] + 1, begin, 0)
+            blank(ping, unit, 0, low0[unit], high0[unit])
+
         for level in range(1, STEPS + 1):
             source, target = (ping, pong) if level % 2 else (pong, ping)
-            low = jnp.maximum(low0 - level, 0)
-            high = jnp.minimum(high0 + level, depth_y - 1)
-
-            def step(y, carry, level=level, source=source, target=target):
+            low = [jnp.maximum(bound - level, 0) for bound in low0]
+            high = [jnp.minimum(bound + level, depth_y - 1) for bound in high0]
+            trips = functools.reduce(
+                jnp.maximum,
+                [(high[unit] - low[unit] + 1 + side[unit]) // (1 + side[unit]) for unit in units],
+            )
+
+            def plane(unit, y, level=level, source=source, target=target):
                 rows = {}
                 carried = {}
                 for x in range(level - 1, extent - level + 1):
-                    rows[x] = source[x, y + pad]
+                    rows[x] = source[unit, x, y + pad]
                     if system:
-                        carried[x] = rows[x] * spread(side, 2, x, y)
+                        carried[x] = rows[x] * spread(side[unit], 2, x, y)
                 for x in range(level, extent - level):
                     here = rows[x]
                     behind, ahead = rows[x - 1], rows[x + 1]
-                    beside = (source[x, y + pad - 1] + source[x, y + pad + 1]) + (turn(here, 1) + turn(here, -1))
+                    beside = (source[unit, x, y + pad - 1] + source[unit, x, y + pad + 1]) + (
+                        turn(here, 1) + turn(here, -1)
+                    )
                     if system:
                         drift = carried[x + 1] - carried[x - 1]
                     else:
-                        drift = spread(side, 2, x, y) * (behind - ahead)
+                        drift = spread(side[unit], 2, x, y) * (behind - ahead)
                     total = beside + (behind + ahead) + drift
                     if system and level == STEPS:
-                        value = spread(side, 0, x, y) * (here * spread(side, 3, x, y)) + total
+                        value = spread(side[unit], 0, x, y) * (here * spread(side[unit], 3, x, y)) + total
                     else:
-                        value = spread(side, 0, x, y) * here + spread(side, 1, x, y) * total
+                        value = spread(side[unit], 0, x, y) * here + spread(side[unit], 1, x, y) * total
                     if level == STEPS:
-                        field[system, x - level, y, group] = value
+                        field[system, x - level, y, unit] = value
                     else:
-                        target[x, y + pad] = value
+                        target[unit, x, y + pad] = value
+
+            def step(trip, carry, low=low, high=high, plane=plane):
+                for unit in units:
+                    span = 1 + side[unit]
+                    for more in range(span):
+                        plane(unit, jnp.minimum(low[unit] + (trip * span + more), high[unit]))
                 return carry
 
-            lax.fori_loop(low, high + 1, step, 0)
-            if level < STEPS:
-                blank(target, level, low, high)
-            else:
-
-                def clear(y, carry):
-                    for x in range(width_x):
-                        field[system, x, y, group] = zero
-                    return carry
-
-                lax.fori_loop(0, low, clear, 0)
-                lax.fori_loop(high + 1, depth_y, clear, 0)
-
-    def main_group(group, carry):
-        at = pl.multiple_of(group * SUB, SUB)
-        for system in range(2):
-            march(
-                system, group, 0,
-                lambda x, system=system: sorted_ref[system, x, pl.ds(at, SUB), :],
-                level_ref[system, pl.ds(at, SUB), :],
-            )
-        return carry
-
-    lax.fori_loop(0, groups, main_group, 0)
-
-    def rim_group(rim, carry):
-        at = pl.multiple_of(rim * SUB, SUB)
-        for system in range(2):
-            march(
-                system, groups + rim, 1,
-                lambda x, system=system: amp[system, x, pl.ds(at, SUB), :],
-                level_ref[system, pl.ds(inputs + at, SUB), :],
-            )
-        return carry
-
-    lax.fori_loop(0, rims, rim_group, 0)
+            lax.fori_loop(0, trips, step, 0)
+            for unit in units:
+                if level < STEPS:
+                    blank(target, unit, level, low[unit], high[unit])
+                else:
+
+                    def clear(y, carry, unit=unit):
+                        for x in range(width_x):
+                            field[system, x, y, unit] = zero
+                        return carry
+
+                    lax.fori_loop(0, low[unit], clear, 0)
+                    lax.fori_loop(high[unit] + 1, depth_y, clear, 0)
+
+    for system in range(2):
+        march(system)
 
     total_ref[...] = jnp.zeros_like(total_ref)
     pairs = depth_y // 2
@@ -284,7 +297,7 @@
         )
         return carry
 
-    lax.fori_loop(0, width_x * pairs, fold, 0)
+    lax.fori_loop(0, width_x * pairs, fold, 0, unroll=4)
 
     def part(row, column):
         return total_ref[row * inputs : (row + 1) * inputs, column * inputs : (column + 1) * inputs]
@@ -296,19 +309,38 @@
 
 def eliminate(matrix):
     size = matrix.shape[0]
-    row_ids = lax.broadcasted_iota(jnp.int32, (size, 2 * size), 0)
-    column_ids = lax.broadcasted_iota(jnp.int32, (size, 2 * size), 1)
-    unit = jnp.where(column_ids - size == row_ids, 1.0, 0.0)
-    work = jnp.where(column_ids < size, jnp.concatenate([matrix, matrix], axis=1), unit)
-    pivots = jnp.ones((size, 1), jnp.float32)
-    ids = lax.broadcasted_iota(jnp.int32, (size, 1), 0)
+    tiles = size // SUB
+    row_ids = lax.broadcasted_iota(jnp.int32, (SUB, LANES), 0)
+    columns = {}
+    for j in range(size):
+        for tile in range(j // SUB, tiles):
+            part = matrix[tile * SUB : (tile + 1) * SUB, j : j + 1]
+            columns[j, tile] = jnp.broadcast_to(part, (SUB, LANES))
+    lanes = lane_ids((SUB, LANES))
+    inverse = [jnp.where(lanes - tile * SUB == row_ids, 1.0, 0.0) for tile in range(tiles)]
+    pivots = [jnp.ones((SUB, LANES), jnp.float32) for tile in range(tiles)]
+
+    def pick(tile, row):
+        return jnp.broadcast_to(tile[row : row + 1, :], (SUB, LANES))
+
     for k in range(size):
-        row = work[k : k + 1, :]
-        pivot = work[k : k + 1, k : k + 1]
-        pivots = jnp.where(ids == k, pivot, pivots)
-        factor = jnp.where(ids > k, work[:, k : k + 1] / pivot, 0.0)
-        work = work - factor * row
-    return work[:, size:], pivots
+        home, place = k // SUB, k % SUB
+        pivot = pick(columns[k, home], place)
+        pivots[home] = jnp.where(row_ids == place, pivot, pivots[home])
+        reciprocal = 1.0 / pivot
+        factors = {}
+        for tile in range(home, tiles):
+            factors[tile] = columns[k, tile] * reciprocal
+        factors[home] = jnp.where(row_ids > place, factors[home], 0.0)
+        for j in range(k + 1, size):
+            across = pick(columns[k, j // SUB], j % SUB)
+            for tile in range(j // SUB, tiles):
+                columns[j, tile] = columns[j, tile] - factors[tile] * across
+        source = pick(inverse[home], place)
+        for tile in range(home, tiles):
+            inverse[tile] = inverse[tile] - factors[tile] * source
+    lower = jnp.concatenate(inverse, axis=0)[:, :size]
+    return lower, jnp.concatenate(pivots, axis=0)[:, :size]
 
 
 def product(left, right, contract):
@@ -362,7 +394,7 @@
                 ]
             return carry
 
-        lax.fori_loop(0, width_x * pairs, project, 0, unroll=4)
+        lax.fori_loop(0, width_x * pairs, project, 0, unroll=8)
 
 
 def ordering(height):
@@ -374,6 +406,30 @@
     rank = jnp.sum(ahead.astype(jnp.int32), axis=1)
     ordered = jnp.sum(jnp.where(rank[None, :] == at[:, None], height[None, :], 0), axis=1)
     return rank, ordered
+
+
+def everywhere(value, wide, narrow):
+    axes = ("wide", "narrow")
+    count = wide * narrow
+    if count & (count - 1):
+        return lax.psum(value, axes)
+    bits = [narrow << i for i in range(wide.bit_length() - 1)]
+    bits += [1 << i for i in range(narrow.bit_length() - 1)]
+
+    def other(value, bit):
+        return lax.ppermute(value, axes, [(i, i ^ bit) for i in range(count)])
+
+    if bits:
+        value = value + other(value, bits[0])
+    rest = bits[1:]
+    for at in range(0, len(rest), 2):
+        pair = rest[at : at + 2]
+        if len(pair) == 1:
+            value = value + other(value, pair[0])
+        else:
+            first, second = pair
+            value = (value + other(value, first)) + (other(value, second) + other(value, first ^ second))
+    return value
 
 
 def on_device(
@@ -400,10 +456,18 @@
 
     flat_in = input_amplitude.reshape(-1, width_z)
     flat_out = output_amplitude.reshape(-1, width_z)
-    sent = jnp.concatenate(
-        [flat_in, flat_out]
-        + [cell.reshape(-1, width_z) for cell in (diffusivity, velocity, damping)]
-    )
+    pieces = [flat_in, flat_out] + [
+        cell.reshape(-1, width_z) for cell in (diffusivity, velocity, damping)
+    ]
+    sent = pl.pallas_call(
+        stage_kernel,
+        out_shape=jax.ShapeDtypeStruct((sum(piece.shape[0] for piece in pieces), width_z), f32),
+        in_specs=[pl.BlockSpec(memory_space=pltpu.HBM)] * len(pieces),
+        out_specs=VMEM,
+        scratch_shapes=[pltpu.SemaphoreType.DMA((len(pieces),))],
+        compiler_params=pltpu.CompilerParams(vmem_limit_bytes=60 * 1024 * 1024),
+        name="stage",
+    )(*pieces)
     near_pairs, far_pairs = swaps(wide)
     near = lax.ppermute(sent, "wide", near_pairs)
     far = lax.ppermute(sent, "wide", far_pairs)
@@ -439,10 +503,11 @@
             jax.ShapeDtypeStruct((3, extent, depth_y, LANES), f32),
             jax.ShapeDtypeStruct((rim_count, SUB, LANES), f32),
         ),
-        in_specs=[SMEM, SMEM] + [VMEM] * 7,
+        in_specs=[SMEM, SMEM] + [VMEM] * 3,
         out_specs=(VMEM, VMEM, VMEM),
+        compiler_params=pltpu.CompilerParams(vmem_limit_bytes=8 << 20),
         name="pack",
-    )(place, ranks, flat_in, flat_out, diffusivity, velocity, damping, near, far)
+    )(place, ranks, sent, near, far)
 
     if narrow == 2:
         from_right = lax.ppermute(rim, "narrow", [(0, 1), (1, 0)])
@@ -465,23 +530,17 @@
         out_specs=(VMEM, VMEM, VMEM),
         scratch_shapes=[
             pltpu.VMEM((2, extent, rims * SUB, LANES), f32),
-            pltpu.VMEM((2, 4, extent, depth_y, LANES), f32),
-            pltpu.VMEM((extent, depth_y + 4, SUB, LANES), f32),
-            pltpu.VMEM((extent, depth_y + 4, SUB, LANES), f32),
+            pltpu.VMEM((2, 4, extent, depth_y, SUB, LANES), f32),
+            pltpu.VMEM((groups + rims, extent, depth_y + 4, SUB, LANES), f32),
+            pltpu.VMEM((groups + rims, extent, depth_y + 4, SUB, LANES), f32),
             pltpu.VMEM((2, width_x, depth_y, groups + rims, SUB, LANES), f32),
             pltpu.VMEM((3 * inputs, 3 * inputs), f32),
         ],
+        compiler_params=pltpu.CompilerParams(vmem_limit_bytes=34 << 20),
         name="window",
     )(bounds, flags, arranged, cells, rim, from_right, from_left, levels)
 
-    step = 1
-    while step < wide:
-        gram = gram + lax.ppermute(gram, "wide", [(i, i ^ step) for i in range(wide)])
-        step *= 2
-    step = 1
-    while step < narrow:
-        gram = gram + lax.ppermute(gram, "narrow", [(i, i ^ step) for i in range(narrow)])
-        step *= 2
+    gram = everywhere(gram, wide, narrow)
 
     scale = 1.0 / math.sqrt(width_x * wide * depth_y * width_z * narrow)
     shape = jax.ShapeDtypeStruct((rank_count * width_x * depth_y, LANES), f32)
@@ -491,6 +550,7 @@
         in_specs=[SMEM] + [VMEM] * 4,
         out_specs=(VMEM, VMEM),
         scratch_shapes=[pltpu.VMEM((inputs, rank_count), f32)],
+        compiler_params=pltpu.CompilerParams(vmem_limit_bytes=7 << 20),
         name="modes",
     )(ranks, gram, start_block, direct, adjoint)
     full = (rank_count, width_x, depth_y, width_z)

time: 143 us -> 85.3 us (0.60)
  Pallas kernels: 96.1 us -> 42.3 us
  other arithmetic: 7.75 us -> 3.67 us
  local copies, waits for them, and re-layouts: 8 us -> 5.02 us
  starting transfers between devices: 16.9 us -> 19.1 us
    pallas_call x1, Pallas kernels: 74.2 us -> 30.9 us  [on_device(): pl.pallas_call(functools.partial(window_kernel, inputs, width_x, depth_y)...]
    pallas_call x1, Pallas kernels: 17.3 us -> 7.48 us  [on_device(): pl.pallas_call(functools.partial(modes_kernel, inputs, width_x, depth_y,...]
    pallas_call x1, Pallas kernels: 4.61 us -> 2.15 us  [on_device(): pl.pallas_call(functools.partial(pack_kernel, inputs, width_x, depth_y),...]
    ppermute x5 -> x7, starting transfers between devices: 10.2 us -> 12.5 us  [other(): return lax.ppermute(value, axes, [(i, i ^ bit) for i in range(count)])]
    unnamed x15 -> x11, local copies, waits for them, and re-layouts: 6.23 us -> 4.01 us
    pallas_call x0 -> x1, Pallas kernels: none -> 1.75 us  [on_device(): pl.pallas_call(stage_kernel, out_shape=jax.ShapeDtypeStruct((sum((piece.s...]
    ppermute x5 -> x7, waiting for transfers between devices: 8.63 us -> 8.98 us  [other(): return lax.ppermute(value, axes, [(i, i ^ bit) for i in range(count)])]
  transfers between devices with their start and end apart: 8 -> 10, of which waited for: 6 -> 8; matrix products, arithmetic and copies ran while one was open for 6% -> 6% of each run, Pallas kernels for 0% -> 0%
where the time goes in v1:
time: 85.3 us; the launch traced here: 85 us
  Pallas kernels  42.3 us (50%)
  starting transfers between devices  19.1 us (22%)
  waiting for transfers between devices  14.1 us (17%)
  local copies, waits for them, and re-layouts  5.02 us (6%)
  other arithmetic  3.67 us (4%)
    pallas_call x1, Pallas kernels, on_device(): pl.pallas_call(functools.partial(window_kernel, inputs, width_x, depth_y)...  30.9 us
    ppermute x7, starting transfers between devices, other(): return lax.ppermute(value, axes, [(i, i ^ bit) for i in range(count)])  12.5 us
    ppermute x7, waiting for transfers between devices, other(): return lax.ppermute(value, axes, [(i, i ^ bit) for i in range(count)])  8.98 us
    pallas_call x1, Pallas kernels, on_device(): pl.pallas_call(functools.partial(modes_kernel, inputs, width_x, depth_y,...  7.48 us
    ppermute x1, waiting for transfers between devices, on_device(): from_right = lax.ppermute(rim, 'narrow', [(0, 1), (1, 0)])  5.13 us
    ppermute x1, starting transfers between devices, on_device(): near = lax.ppermute(sent, 'wide', near_pairs)  4.37 us
    unnamed x11, local copies, waits for them, and re-layouts  4.01 us
    pallas_call x1, Pallas kernels, on_device(): pl.pallas_call(functools.partial(pack_kernel, inputs, width_x, depth_y),...  2.15 us
  transfers between devices with their start and end apart: 10, of which 8 were waited for; matrix products, arithmetic and copies ran while one was open for 6% of the time, Pallas kernels for 0%

profile of v1, /device:TPU:0, one launch (start us, length us, event | category | flops | bytes accessed | tf_op | source)
XLA Modules:
  0.0 85.0 jit_solution(17500054104232184363)
XLA Ops:
  0.6 1.8 %stage.1.here = f32[704,128]{1,0:T(8,128)} custom-call(f32[256,128]{1,0:T(8,128)} %bitcast.17, f32[256,128]{1,0:T(8,128)} %bitcast.18, f32[64,128]{1,0:T(8,128)} %bitcast.19, f32[64,128]{1,0:T(8,128)} %bitcast.20, f32[64,128]{1,0:T(8,128)} %bitcast.21), custom_call_target="tpu_custom_call" | custom-call | tf_op jit(solution)/shard_map/stage/pallas_call | solution.py:462
  2.4 0.0 copy-start.3
  2.4 0.7 collective-permute-start.1
  3.1 4.4 %collective-permute-start = (f32[704,128]{1,0:T(8,128)}, f32[704,128]{1,0:T(8,128)S(1)}, u32[]{:S(2)}, u32[]{:S(2)}) collective-permute-start(f32[704,128]{1,0:T(8,128)} %stage.1.here), channel_id=1, source_target_pairs={{0,2},{2,0},{4,6},{6,4},{8,10},{10,8},{12,14},{14,12},{16,18},{18,... | collective-permute-start | bytes 1081352 | tf_op jit(solution)/shard_map/ppermute | solution.py:472
  7.5 0.9 %convert_reduce_fusion = s32[64]{0:T(128)S(1)} fusion(s32[64]{0:T(128)} %param.14), kind=kLoop, calls=%fused_computation.7 | loop fusion | flops 28608 | bytes 512 | tf_op jit(solution)/shard_map/reduce_sum | solution.py:406
  8.4 0.8 select_reduce_fusion
  9.2 0.1 stack.72
  9.2 0.1 stack.86
  9.3 0.9 %convert_reduce_fusion.1 = s32[64]{0:T(128)S(1)} fusion(s32[64]{0:T(128)} %param.13), kind=kLoop, calls=%fused_computation.8 | loop fusion | flops 28608 | bytes 512 | tf_op jit(solution)/shard_map/reduce_sum | solution.py:406
  10.2 0.8 select_reduce_fusion.1
  11.0 0.1 stack.71
  11.1 0.1 stack.85
  11.2 0.1 stack.67
  11.3 0.1 fusion.5
  11.4 0.1 pad_add_fusion.3.place_ref
  11.5 0.1 stack.68
  11.6 0.1 copy.23
  11.7 0.1 broadcast_in_dim.20
  11.8 0.1 reshape_reshape.3
  11.9 0.1 fusion.4
  12.0 0.0 collective-permute-done.1.far
  12.0 0.0 collective-permute-done.near
  12.0 1.0 %copy-done.2 = f32[704,128]{1,0:T(8,128)S(1)} copy-done((f32[704,128]{1,0:T(8,128)S(1)}, f32[704,128]{1,0:T(8,128)}, u32[]{:S(2)}) %copy-start.2) | copy-done | bytes 360472
  13.0 2.1 %pack.1 = (f32[2,12,64,128]{3,2,1,0:T(8,128)S(1)}, f32[3,12,16,128]{3,2,1,0:T(8,128)S(1)}, f32[72,8,128]{2,1,0:T(8,128)S(1)}) custom-call(s32[2]{0:T(128)S(1)} %pad_add_fusion.3.place_ref, s32[2,64]{1,0:T(2,128)S(1)} %pad_add_fusion.1.rank_ref, f32[704,128]{1,0:T(8,128)S(1)} %copy-done.2, f32[704,128]{1,0:T(8,128)S(1)} %collective-permute-done.near, ...), custom_call_target="tpu_custom_call" | custom-call | tf_op jit(solution)/shard_map/pack/pallas_call | solution.py:499
  15.1 1.6 %collective-permute-start.2 = (f32[72,8,128]{2,1,0:T(8,128)S(1)}, f32[72,8,128]{2,1,0:T(8,128)S(1)}, u32[]{:S(2)}, u32[]{:S(2)}) collective-permute-start(f32[72,8,128]{2,1,0:T(8,128)S(1)} %get-tuple-element.12.rim_ref), channel_id=1, source_target_pairs={{0,1},{1,0},{2,3},{3,2},{4,5},{5,4},{6,7},{7,6},{8,9},{9,8},{10,11... | collective-permute-start | bytes 884744 | tf_op jit(solution)/shard_map/ppermute | solution.py:513
  16.7 0.1 add_convert_fusion.flag_ref
  16.8 0.1 add_add_fusion.2.bounds_ref
  16.8 0.1 broadcast_in_dim.19
  16.9 5.1 %collective-permute-done.2.from_right.from_left = f32[72,8,128]{2,1,0:T(8,128)S(1)} collective-permute-done((f32[72,8,128]{2,1,0:T(8,128)S(1)}, f32[72,8,128]{2,1,0:T(8,128)S(1)}, u32[]{:S(2)}, u32[]{:S(2)}) %collective-permute-start.2) | collective-permute-done | bytes 294944 | tf_op jit(solution)/shard_map/ppermute | solution.py:513
  22.1 30.9 %window.1 = (bf16[32,128,256]{2,1,0:T(8,128)(2,1)S(1)}, bf16[32,128,256]{2,1,0:T(8,128)(2,1)S(1)}, f32[64,64]{1,0:T(8,128)S(1)}) custom-call(s32[2,10,2]{2,1,0:T(8,128)S(1)} %add_add_fusion.2.bounds_ref, s32[2]{0:T(128)S(1)} %add_convert_fusion.flag_ref, f32[2,12,64,128]{3,2,1,0:T(8,128)S(1)} %get-tuple-element.10.sorted_ref, ...), custom_call_target="tpu_custom_call" | custom-call | tf_op jit(solution)/shard_map/window/pallas_call | solution.py:522
  52.9 1.4 %copy-done = bf16[32,128,256]{2,1,0:T(8,128)(2,1)} copy-done((bf16[32,128,256]{2,1,0:T(8,128)(2,1)}, bf16[32,128,256]{2,1,0:T(8,128)(2,1)S(1)}, u32[]{:S(2)}) %copy-start) | copy-done | bytes 2097176
  54.3 2.8 %collective-permute-start.3 = (f32[64,64]{1,0:T(8,128)S(1)}, f32[64,64]{1,0:T(8,128)S(1)}, u32[]{:S(2)}, u32[]{:S(2)}) collective-permute-start(f32[64,64]{1,0:T(8,128)S(1)} %get-tuple-element.13), channel_id=1, source_target_pairs={{0,2},{1,3},{2,0},{3,1},{4,6},{5,7},{6,4},{7,5},{8,10},{9,11},{10,... | collective-permute-start | bytes 49160 | tf_op jit(solution)/shard_map/ppermute | solution.py:420
  57.1 0.9 %collective-permute-done.3 = f32[64,64]{1,0:T(8,128)S(1)} collective-permute-done((f32[64,64]{1,0:T(8,128)S(1)}, f32[64,64]{1,0:T(8,128)S(1)}, u32[]{:S(2)}, u32[]{:S(2)}) %collective-permute-start.3) | collective-permute-done | bytes 16416 | tf_op jit(solution)/shard_map/ppermute | solution.py:420
  58.0 4.6 %collective-permute-start.6 = (f32[64,64]{1,0:T(8,128)S(1)}, f32[64,64]{1,0:T(8,128)S(1)}, u32[]{:S(2)}, u32[]{:S(2)}) collective-permute-start(f32[64,64]{1,0:T(8,128)S(1)} %add.30), channel_id=1, source_target_pairs={{0,12},{1,13},{2,14},{3,15},{4,8},{5,9},{6,10},{7,11},{8,4},{9,5},... | collective-permute-start | bytes 49160 | tf_op jit(solution)/shard_map/ppermute | solution.py:420
  62.6 0.5 collective-permute-start.5
  63.0 0.2 collective-permute-start.4
  63.2 1.3 %collective-permute-done.6 = f32[64,64]{1,0:T(8,128)S(1)} collective-permute-done((f32[64,64]{1,0:T(8,128)S(1)}, f32[64,64]{1,0:T(8,128)S(1)}, u32[]{:S(2)}, u32[]{:S(2)}) %collective-permute-start.6) | collective-permute-done | bytes 16416 | tf_op jit(solution)/shard_map/ppermute | solution.py:420
  64.5 2.0 %collective-permute-done.5 = f32[64,64]{1,0:T(8,128)S(1)} collective-permute-done((f32[64,64]{1,0:T(8,128)S(1)}, f32[64,64]{1,0:T(8,128)S(1)}, u32[]{:S(2)}, u32[]{:S(2)}) %collective-permute-start.5) | collective-permute-done | bytes 16416 | tf_op jit(solution)/shard_map/ppermute | solution.py:420
  66.5 0.5 collective-permute-done.4
  67.0 3.6 %collective-permute-start.9 = (f32[64,64]{1,0:T(8,128)S(1)}, f32[64,64]{1,0:T(8,128)S(1)}, u32[]{:S(2)}, u32[]{:S(2)}) collective-permute-start(f32[64,64]{1,0:T(8,128)S(1)} %add_add_fusion.1), channel_id=1, source_target_pairs={{0,17},{1,16},{2,19},{3,18},{4,21},{5,20},{6,23},{7,22},{8,25},{9,... | collective-permute-start | bytes 49160 | tf_op jit(solution)/shard_map/ppermute | solution.py:420
  70.6 0.5 collective-permute-start.8
  71.1 0.3 collective-permute-start.7
  71.4 0.1 copy.24.start_ref
  71.5 1.2 %collective-permute-done.9 = f32[64,64]{1,0:T(8,128)S(1)} collective-permute-done((f32[64,64]{1,0:T(8,128)S(1)}, f32[64,64]{1,0:T(8,128)S(1)}, u32[]{:S(2)}, u32[]{:S(2)}) %collective-permute-start.9) | collective-permute-done | bytes 16416 | tf_op jit(solution)/shard_map/ppermute | solution.py:420
  72.7 1.7 %collective-permute-done.8 = f32[64,64]{1,0:T(8,128)S(1)} collective-permute-done((f32[64,64]{1,0:T(8,128)S(1)}, f32[64,64]{1,0:T(8,128)S(1)}, u32[]{:S(2)}, u32[]{:S(2)}) %collective-permute-start.8) | collective-permute-done | bytes 16416 | tf_op jit(solution)/shard_map/ppermute | solution.py:420
  74.5 1.4 %collective-permute-done.7 = f32[64,64]{1,0:T(8,128)S(1)} collective-permute-done((f32[64,64]{1,0:T(8,128)S(1)}, f32[64,64]{1,0:T(8,128)S(1)}, u32[]{:S(2)}, u32[]{:S(2)}) %collective-permute-start.7) | collective-permute-done | bytes 16416 | tf_op jit(solution)/shard_map/ppermute | solution.py:420
  75.9 1.6 %copy-done.1 = bf16[32,128,256]{2,1,0:T(8,128)(2,1)S(1)} copy-done((bf16[32,128,256]{2,1,0:T(8,128)(2,1)S(1)}, bf16[32,128,256]{2,1,0:T(8,128)(2,1)}, u32[]{:S(2)}) %copy-start.1) | copy-done | bytes 2097176
  77.5 7.5 %modes.1 = (f32[2048,128]{1,0:T(8,128)}, f32[2048,128]{1,0:T(8,128)}) custom-call(s32[2,64]{1,0:T(2,128)S(1)} %pad_add_fusion.1.rank_ref, f32[64,64]{1,0:T(8,128)S(1)} %add_add_fusion.gram_ref, f32[64,32]{1,0:T(8,128)S(1)} %copy.24.start_ref, bf16[32,128,256]{2,1,0:T(8,128)(2,1)S(1)} %get-tuple-element.14.direct_ref, bf16[32,128,256]{2,1,0:T(8,128)(2,1)S(1)} %copy-done.1), custom_call_target="tpu_custom_call" | custom-call | tf_op jit(solution)/shard_map/modes/pallas_call | solution.py:547
  (15 shorter events, 0.1 us)
Async XLA Ops:
  2.4 69.0 %copy-start.3 = (f32[64,32]{0,1:T(8,128)S(1)}, f32[64,32]{0,1:T(8,128)}, u32[]{:S(2)}) copy-start(f32[64,32]{0,1:T(8,128)} %param.15) | copy-start | bytes 24580
  2.4 9.6 %collective-permute-start.1 = (f32[704,128]{1,0:T(8,128)}, f32[704,128]{1,0:T(8,128)S(1)}, u32[]{:S(2)}, u32[]{:S(2)}) collective-permute-start(f32[704,128]{1,0:T(8,128)} %stage.1.here), channel_id=1, source_target_pairs={{2,4},{4,2},{6,8},{8,6},{10,12},{12,10},{14,16},{16,14},{18,20},{2... | collective-permute-start | bytes 1081352 | tf_op jit(solution)/shard_map/ppermute | solution.py:473
  3.1 8.9 %collective-permute-start = (f32[704,128]{1,0:T(8,128)}, f32[704,128]{1,0:T(8,128)S(1)}, u32[]{:S(2)}, u32[]{:S(2)}) collective-permute-start(f32[704,128]{1,0:T(8,128)} %stage.1.here), channel_id=1, source_target_pairs={{0,2},{2,0},{4,6},{6,4},{8,10},{10,8},{12,14},{14,12},{16,18},{18,... | collective-permute-start | bytes 1081352 | tf_op jit(solution)/shard_map/ppermute | solution.py:472
  12.0 1.0 %copy-start.2 = (f32[704,128]{1,0:T(8,128)S(1)}, f32[704,128]{1,0:T(8,128)}, u32[]{:S(2)}) copy-start(f32[704,128]{1,0:T(8,128)} %stage.1.here) | copy-start | bytes 1081348
  15.1 7.0 %collective-permute-start.2 = (f32[72,8,128]{2,1,0:T(8,128)S(1)}, f32[72,8,128]{2,1,0:T(8,128)S(1)}, u32[]{:S(2)}, u32[]{:S(2)}) collective-permute-start(f32[72,8,128]{2,1,0:T(8,128)S(1)} %get-tuple-element.12.rim_ref), channel_id=1, source_target_pairs={{0,1},{1,0},{2,3},{3,2},{4,5},{5,4},{6,7},{7,6},{8,9},{9,8},{10,11... | collective-permute-start | bytes 884744 | tf_op jit(solution)/shard_map/ppermute | solution.py:513
  52.9 1.4 %copy-start = (bf16[32,128,256]{2,1,0:T(8,128)(2,1)}, bf16[32,128,256]{2,1,0:T(8,128)(2,1)S(1)}, u32[]{:S(2)}) copy-start(bf16[32,128,256]{2,1,0:T(8,128)(2,1)S(1)} %get-tuple-element.15.adjoint_ref) | copy-start | bytes 6291460
  54.3 3.7 %collective-permute-start.3 = (f32[64,64]{1,0:T(8,128)S(1)}, f32[64,64]{1,0:T(8,128)S(1)}, u32[]{:S(2)}, u32[]{:S(2)}) collective-permute-start(f32[64,64]{1,0:T(8,128)S(1)} %get-tuple-element.13), channel_id=1, source_target_pairs={{0,2},{1,3},{2,0},{3,1},{4,6},{5,7},{6,4},{7,5},{8,10},{9,11},{10,... | collective-permute-start | bytes 49160 | tf_op jit(solution)/shard_map/ppermute | solution.py:420
  58.0 6.5 %collective-permute-start.6 = (f32[64,64]{1,0:T(8,128)S(1)}, f32[64,64]{1,0:T(8,128)S(1)}, u32[]{:S(2)}, u32[]{:S(2)}) collective-permute-start(f32[64,64]{1,0:T(8,128)S(1)} %add.30), channel_id=1, source_target_pairs={{0,12},{1,13},{2,14},{3,15},{4,8},{5,9},{6,10},{7,11},{8,4},{9,5},... | collective-permute-start | bytes 49160 | tf_op jit(solution)/shard_map/ppermute | solution.py:420
  62.6 3.9 %collective-permute-start.5 = (f32[64,64]{1,0:T(8,128)S(1)}, f32[64,64]{1,0:T(8,128)S(1)}, u32[]{:S(2)}, u32[]{:S(2)}) collective-permute-start(f32[64,64]{1,0:T(8,128)S(1)} %add.30), channel_id=1, source_target_pairs={{0,8},{1,9},{2,10},{3,11},{4,12},{5,13},{6,14},{7,15},{8,0},{9,1},... | collective-permute-start | bytes 49160 | tf_op jit(solution)/shard_map/ppermute | solution.py:420
  63.0 3.9 %collective-permute-start.4 = (f32[64,64]{1,0:T(8,128)S(1)}, f32[64,64]{1,0:T(8,128)S(1)}, u32[]{:S(2)}, u32[]{:S(2)}) collective-permute-start(f32[64,64]{1,0:T(8,128)S(1)} %add.30), channel_id=1, source_target_pairs={{0,4},{1,5},{2,6},{3,7},{4,0},{5,1},{6,2},{7,3},{8,12},{9,13},{10,... | collective-permute-start | bytes 49160 | tf_op jit(solution)/shard_map/ppermute | solution.py:420
  67.0 5.8 %collective-permute-start.9 = (f32[64,64]{1,0:T(8,128)S(1)}, f32[64,64]{1,0:T(8,128)S(1)}, u32[]{:S(2)}, u32[]{:S(2)}) collective-permute-start(f32[64,64]{1,0:T(8,128)S(1)} %add_add_fusion.1), channel_id=1, source_target_pairs={{0,17},{1,16},{2,19},{3,18},{4,21},{5,20},{6,23},{7,22},{8,25},{9,... | collective-permute-start | bytes 49160 | tf_op jit(solution)/shard_map/ppermute | solution.py:420
  70.6 3.9 %collective-permute-start.8 = (f32[64,64]{1,0:T(8,128)S(1)}, f32[64,64]{1,0:T(8,128)S(1)}, u32[]{:S(2)}, u32[]{:S(2)}) collective-permute-start(f32[64,64]{1,0:T(8,128)S(1)} %add_add_fusion.1), channel_id=1, source_target_pairs={{0,1},{1,0},{2,3},{3,2},{4,5},{5,4},{6,7},{7,6},{8,9},{9,8},{10,11... | collective-permute-start | bytes 49160 | tf_op jit(solution)/shard_map/ppermute | solution.py:420
  71.1 4.8 %collective-permute-start.7 = (f32[64,64]{1,0:T(8,128)S(1)}, f32[64,64]{1,0:T(8,128)S(1)}, u32[]{:S(2)}, u32[]{:S(2)}) collective-permute-start(f32[64,64]{1,0:T(8,128)S(1)} %add_add_fusion.1), channel_id=1, source_target_pairs={{0,16},{1,17},{2,18},{3,19},{4,20},{5,21},{6,22},{7,23},{8,24},{9,... | collective-permute-start | bytes 49160 | tf_op jit(solution)/shard_map/ppermute | solution.py:420
  75.9 1.6 %copy-start.1 = (bf16[32,128,256]{2,1,0:T(8,128)(2,1)S(1)}, bf16[32,128,256]{2,1,0:T(8,128)(2,1)}, u32[]{:S(2)}) copy-start(bf16[32,128,256]{2,1,0:T(8,128)(2,1)} %copy-done) | copy-start | bytes 6291460

commit v2 on v1

--- a/solution.py
+++ b/solution.py
@@ -17,6 +17,7 @@
 LEFT = 0
 RIGHT = 16
 REACH = STEPS + SUB
+PAD = STEPS + 1
 
 VMEM = pl.BlockSpec(memory_space=pltpu.VMEM)
 SMEM = pl.BlockSpec(memory_space=pltpu.SMEM)
@@ -118,11 +119,155 @@
     return first, second, third
 
 
-def window_kernel(
+def store_cells(coef, x, tile, diff, vel, damp):
+    inverse = jnp.where(diff > 0.0, 1.0 / jnp.where(diff > 0.0, diff, 1.0), 0.0)
+    for which, value in enumerate((1.0 - 6.0 * diff - damp, diff, vel, inverse)):
+        for y in range(SUB):
+            coef[which, x, tile * SUB + y] = jnp.broadcast_to(value[y : y + 1, :], (SUB, LANES))
+
+
+def march(units, share, depth_y, extent, bounds, load, heights, coef, ping, pong, write, wipe):
+    zero = jnp.zeros((SUB, LANES), jnp.float32)
+    count = len(units)
+    low0 = [bounds[system, row, 0] for system, row in units]
+    high0 = [bounds[system, row, 1] for system, row in units]
+    top = depth_y - 1
+
+    for at in range(count):
+        levels = heights(at)
+        for x in range(extent):
+            for buffer in (ping, pong):
+                buffer[at, x, PAD - 1] = zero
+                buffer[at, x, PAD + depth_y] = zero
+
+        def begin(y, carry, at=at, levels=levels):
+            here = levels == y
+            for x in range(extent):
+                value = jnp.where(here, load(at, x), 0.0)
+                if units[at][0]:
+                    value = value * coef[1, x, y]
+                ping[at, x, y + PAD] = value
+            return carry
+
+        lax.fori_loop(low0[at], high0[at] + 1, begin, 0)
+        for x in range(1, extent - 1):
+            ping[at, x, low0[at] - 1 + PAD] = zero
+            ping[at, x, high0[at] + 1 + PAD] = zero
+
+    for level in range(1, STEPS + 1):
+        source, target = (ping, pong) if level % 2 else (pong, ping)
+        low = [jnp.maximum(bound - level + 1, 0) for bound in low0]
+        high = [jnp.minimum(bound + level - 1, top) for bound in high0]
+        trips = functools.reduce(
+            jnp.maximum, [(high[at] - low[at] + share) // share for at in range(count)]
+        )
+
+        def plane(at, y, level=level, source=source, target=target):
+            system = units[at][0]
+            rows = {}
+            carried = {}
+            for x in range(level - 1, extent - level + 1):
+                rows[x] = source[at, x, y + PAD]
+                if system:
+                    carried[x] = rows[x] * coef[2, x, y]
+            for x in range(level, extent - level):
+                here = rows[x]
+                behind, ahead = rows[x - 1], rows[x + 1]
+                beside = (source[at, x, y + PAD - 1] + source[at, x, y + PAD + 1]) + (
+                    turn(here, 1) + turn(here, -1)
+                )
+                if system:
+                    drift = carried[x + 1] - carried[x - 1]
+                else:
+                    drift = coef[2, x, y] * (behind - ahead)
+                total = beside + (behind + ahead) + drift
+                if system and level == STEPS:
+                    value = coef[0, x, y] * (here * coef[3, x, y]) + total
+                else:
+                    value = coef[0, x, y] * here + coef[1, x, y] * total
+                if level == STEPS:
+                    write(at, x - level, y, value)
+                else:
+                    target[at, x, y + PAD] = value
+
+        def step(trip, carry, low=low, high=high, plane=plane):
+            for at in range(count):
+                for more in range(share):
+                    plane(at, jnp.minimum(low[at] + (trip * share + more), high[at]))
+            return carry
+
+        lax.fori_loop(0, trips, step, 0)
+        for at in range(count):
+            for y, inner, outer in (
+                (low0[at] - level, 1, -1),
+                (high0[at] + level, -1, 1),
+            ):
+                inside = (y >= 0) & (y <= top)
+                if level < STEPS:
+                    near = jnp.minimum(jnp.maximum(y, 0), top)
+                    for x in range(level, extent - level):
+                        value = coef[1, x, near] * source[at, x, y + inner + PAD]
+                        target[at, x, y + PAD] = jnp.where(inside, value, 0.0)
+                        if level < x < extent - level - 1:
+                            target[at, x, y + outer + PAD] = zero
+                else:
+
+                    @pl.when(inside)
+                    def _(at=at, y=y, inner=inner, level=level, source=source):
+                        for x in range(level, extent - level):
+                            value = source[at, x, y + inner + PAD]
+                            if not units[at][0]:
+                                value = coef[1, x, y] * value
+                            write(at, x - level, y, value)
+
+            if level == STEPS:
+
+                def clear(y, carry, at=at):
+                    wipe(at, y, zero)
+                    return carry
+
+                lax.fori_loop(0, low0[at] - level, clear, 0)
+                lax.fori_loop(high0[at] + level + 1, depth_y, clear, 0)
+
+
+def main_kernel(
+    inputs, width_x, depth_y, bounds_ref, sorted_ref, cell_ref, level_ref, field, coef, ping, pong
+):
+    groups = inputs // SUB
+    extent = 3 * width_x
+
+    def prepare(x, carry):
+        for tile in range(depth_y // SUB):
+            rows = slice(tile * SUB, (tile + 1) * SUB)
+            store_cells(coef, x, tile, *(cell_ref[which, x, rows, :] for which in range(3)))
+        return carry
+
+    lax.fori_loop(0, extent, prepare, 0, unroll=2)
+    units = [(system, group) for system in range(2) for group in range(groups)]
+
+    def rows(at):
+        return slice(units[at][1] * SUB, (units[at][1] + 1) * SUB)
+
+    def write(at, x, y, value):
+        field[units[at][0], x, y, units[at][1]] = value
+
+    def wipe(at, y, zero):
+        for x in range(width_x):
+            write(at, x, y, zero)
+
+    march(
+        units, 1, depth_y, extent, bounds_ref,
+        lambda at, x: sorted_ref[units[at][0], x, rows(at), :],
+        lambda at: level_ref[units[at][0], rows(at), :],
+        coef, ping, pong, write, wipe,
+    )
+
+
+def rim_kernel(
     inputs, width_x, depth_y, bounds_ref, flag_ref,
-    sorted_ref, cell_ref, rim_ref, from_right, from_left, level_ref,
+    rim_ref, from_right, from_left, level_ref, field,
     direct_ref, adjoint_ref, gram_ref,
-    amp, coef, ping, pong, field, total_ref,
+    amp, coef, ping, pong, edge_field, total_ref,
 ):
     groups = inputs // SUB
     rims = groups // PER
@@ -140,16 +285,10 @@
 
     pieces = [(which, tile) for which in range(3) for tile in range(tiles)]
 
-    def put(side, x, tile, diff, vel, damp):
-        inverse = jnp.where(diff > 0.0, 1.0 / jnp.where(diff > 0.0, diff, 1.0), 0.0)
-        for which, value in enumerate((1.0 - 6.0 * diff - damp, diff, vel, inverse)):
-            for y in range(SUB):
-                coef[side, which, x, tile * SUB + y] = jnp.broadcast_to(value[y : y + 1, :], (SUB, LANES))
-
     def prepare(x, carry):
         for system in range(2):
             for rim in range(rims):
-                amp[system, x, rim * SUB : (rim + 1) * SUB, :] = whole_rim((system * rims + rim) * extent + x)
+                amp[system * rims + rim, x] = whole_rim((system * rims + rim) * extent + x)
         parts = {}
         for at in range(0, len(pieces), PER):
             packed = whole_rim((2 * rims + at // PER) * extent + x)
@@ -161,110 +300,28 @@
                     step *= 2
                 parts[piece] = alone
         for tile in range(tiles):
-            rows = slice(tile * SUB, (tile + 1) * SUB)
-            put(0, x, tile, *(cell_ref[which, x, rows, :] for which in range(3)))
-            put(1, x, tile, *(parts[(which, tile)] for which in range(3)))
+            store_cells(coef, x, tile, *(parts[(which, tile)] for which in range(3)))
         return carry
 
     lax.fori_loop(0, extent, prepare, 0, unroll=extent)
-
-    def spread(side, which, x, y):
-        return coef[side, which, x, y]
-
-    pad = 2
-    zero = jnp.zeros((SUB, LANES), jnp.float32)
-
-    def march(system):
-        units = range(groups + rims)
-        side = [int(unit >= groups) for unit in units]
-        low0 = [bounds_ref[system, unit, 0] for unit in units]
-        high0 = [bounds_ref[system, unit, 1] for unit in units]
-
-        def blank(target, unit, margin, low, high):
-            for x in range(margin, extent - margin):
-                for offset in (1, 2):
-                    target[unit, x, low - offset + pad] = zero
-                    target[unit, x, high + offset + pad] = zero
-
-        for unit in units:
-            rows = slice(unit * SUB, (unit + 1) * SUB)
-            heights = level_ref[system, rows, :]
-
-            def begin(y, carry, unit=unit, rows=rows, heights=heights):
-                here = heights == y
-                for x in range(extent):
-                    if side[unit]:
-                        value = amp[system, x, (unit - groups) * SUB : (unit - groups + 1) * SUB, :]
-                    else:
-                        value = sorted_ref[system, x, rows, :]
-                    value = jnp.where(here, value, 0.0)
-                    if system:
-                        value = value * spread(side[unit], 1, x, y)
-                    ping[unit, x, y + pad] = value
-                return carry
-
-            lax.fori_loop(low0[unit], high0[unit] + 1, begin, 0)
-            blank(ping, unit, 0, low0[unit], high0[unit])
-
-        for level in range(1, STEPS + 1):
-            source, target = (ping, pong) if level % 2 else (pong, ping)
-            low = [jnp.maximum(bound - level, 0) for bound in low0]
-            high = [jnp.minimum(bound + level, depth_y - 1) for bound in high0]
-            trips = functools.reduce(
-                jnp.maximum,
-                [(high[unit] - low[unit] + 1 + side[unit]) // (1 + side[unit]) for unit in units],
-            )
-
-            def plane(unit, y, level=level, source=source, target=target):
-                rows = {}
-                carried = {}
-                for x in range(level - 1, extent - level + 1):
-                    rows[x] = source[unit, x, y + pad]
-                    if system:
-                        carried[x] = rows[x] * spread(side[unit], 2, x, y)
-                for x in range(level, extent - level):
-                    here = rows[x]
-                    behind, ahead = rows[x - 1], rows[x + 1]
-                    beside = (source[unit, x, y + pad - 1] + source[unit, x, y + pad + 1]) + (
-                        turn(here, 1) + turn(here, -1)
-                    )
-                    if system:
-                        drift = carried[x + 1] - carried[x - 1]
-                    else:
-                        drift = spread(side[unit], 2, x, y) * (behind - ahead)
-                    total = beside + (behind + ahead) + drift
-                    if system and level == STEPS:
-                        value = spread(side[unit], 0, x, y) * (here * spread(side[unit], 3, x, y)) + total
-                    else:
-                        value = spread(side[unit], 0, x, y) * here + spread(side[unit], 1, x, y) * total
-                    if level == STEPS:
-                        field[system, x - level, y, unit] = value
-                    else:
-                        target[unit, x, y + pad] = value
-
-            def step(trip, carry, low=low, high=high, plane=plane):
-                for unit in units:
-                    span = 1 + side[unit]
-                    for more in range(span):
-                        plane(unit, jnp.minimum(low[unit] + (trip * span + more), high[unit]))
-                return carry
-
-            lax.fori_loop(0, trips, step, 0)
-            for unit in units:
-                if level < STEPS:
-                    blank(target, unit, level, low[unit], high[unit])
-                else:
-
-                    def clear(y, carry, unit=unit):
-                        for x in range(width_x):
-                            field[system, x, y, unit] = zero
-                        return carry
-
-                    lax.fori_loop(0, low[unit], clear, 0)
-                    lax.fori_loop(high[unit] + 1, depth_y, clear, 0)
-
-    for system in range(2):
-        march(system)
+    units = [(system, groups + rim) for system in range(2) for rim in range(rims)]
+
+    def rows(at):
+        return slice(units[at][1] * SUB, (units[at][1] + 1) * SUB)
+
+    def write(at, x, y, value):
+        edge_field[at, x, y] = value
+
+    def wipe(at, y, zero):
+        for x in range(width_x):
+            write(at, x, y, zero)
+
+    march(
+        units, 2, depth_y, extent, bounds_ref,
+        lambda at, x: amp[at, x],
+        lambda at: level_ref[units[at][0], rows(at), :],
+        coef, ping, pong, write, wipe,
+    )
 
     total_ref[...] = jnp.zeros_like(total_ref)
     pairs = depth_y // 2
@@ -277,14 +334,14 @@
             halves = []
             for half in range(2):
                 merged = []
-                for group in range(groups):
-                    edge = field[system, x, y + half, groups + group // PER]
-                    slot = group % PER
-                    value = field[system, x, y + half, group]
-                    low = turn(edge, -(slot * SLOT + LEFT + STEPS))
-                    high = turn(edge, LANES - STEPS - (slot * SLOT + RIGHT + STEPS))
-                    value = jnp.where(lanes < STEPS, low, jnp.where(lanes >= LANES - STEPS, high, value))
-                    merged.append(value)
+                for rim in range(rims):
+                    edge = edge_field[system * rims + rim, x, y + half]
+                    edge = jnp.where(within < LEFT + STEPS, turn(edge, LEFT - RIGHT - STEPS), edge)
+                    for slot in range(PER):
+                        value = field[system, x, y + half, rim * PER + slot]
+                        both = turn(edge, -(slot * SLOT + LEFT + STEPS))
+                        outer = (lanes < STEPS) | (lanes >= LANES - STEPS)
+                        merged.append(jnp.where(outer, both, value))
                 halves.append(jnp.concatenate(merged, axis=0))
             whole = jnp.concatenate(halves, axis=1)
             first, second, third = split(whole)
@@ -350,25 +407,23 @@
 
 
 def modes_kernel(
-    inputs, width_x, depth_y, scale, rank_ref,
-    gram_ref, start_ref, direct_ref, adjoint_ref,
+    inputs, width_x, depth_y, scale,
+    rank_ref, gram_ref, start_ref, direct_ref, adjoint_ref,
     direct_out, adjoint_out,
-    start_sorted,
+    direct_hold, sem,
 ):
-    modes = start_ref.shape[1]
-
-    def move(j, carry):
-        start_sorted[pl.ds(rank_ref[0, j], 1), :] = start_ref[pl.ds(j, 1), :]
-        return carry
-
-    lax.fori_loop(0, inputs, move, 0, unroll=8)
+    modes = start_ref.shape[0]
+
+    ids = lax.broadcasted_iota(jnp.int32, (inputs, inputs), 0)
+    chosen = jnp.where(rank_ref[0:1, :] == ids, 1.0, 0.0)
+    start_sorted = product(chosen, start_ref[...], ((1,), (1,)))
     gram = gram_ref[...] * scale
 
     def orthonormal(block):
         lower, pivots = eliminate(product(block, block, ((0,), (0,))))
         return product(block, lower * lax.rsqrt(pivots), ((1,), (1,)))
 
-    first = orthonormal(product(gram, start_sorted[...], ((1,), (0,))))
+    first = orthonormal(product(gram, start_sorted, ((1,), (0,))))
     right = orthonormal(product(gram, first, ((0,), (0,))))
     reached = product(gram, right, ((1,), (0,)))
     lower, pivots = eliminate(product(reached, reached, ((0,), (0,))))
@@ -379,7 +434,7 @@
         product(lower / (root * quarter), reached, ((1,), (1,))),
     )
     pairs = depth_y // 2
-    for mix, source, out in zip(mixes, (direct_ref, adjoint_ref), (direct_out, adjoint_out)):
+    for mix, source, out in zip(mixes, (direct_ref, adjoint_ref), (direct_hold, adjoint_out)):
         high, low, rest = split(mix)
         stacked = jnp.concatenate(
             [jnp.concatenate([high, high], axis=1), jnp.concatenate([low, low], axis=1)], axis=0
@@ -395,6 +450,10 @@
             return carry
 
         lax.fori_loop(0, width_x * pairs, project, 0, unroll=8)
+        if out is direct_hold:
+            leave = pltpu.make_async_copy(direct_hold, direct_out, sem)
+            leave.start()
+    leave.wait()
 
 
 def ordering(height):
@@ -519,26 +578,43 @@
     flags = jnp.stack([(side + 1 < narrow).astype(jnp.int32), (side > 0).astype(jnp.int32)])
 
     pair_count = width_x * depth_y // 2
+    cells_all = extent * depth_y
+    field = pl.pallas_call(
+        functools.partial(main_kernel, inputs, width_x, depth_y),
+        out_shape=jax.ShapeDtypeStruct((2, width_x, depth_y, groups, SUB, LANES), f32),
+        in_specs=[SMEM] + [VMEM] * 3,
+        out_specs=VMEM,
+        scratch_shapes=[
+            pltpu.VMEM((4, extent, depth_y, SUB, LANES), f32),
+            pltpu.VMEM((2 * groups, extent, depth_y + 2 * PAD, SUB, LANES), f32),
+            pltpu.VMEM((2 * groups, extent, depth_y + 2 * PAD, SUB, LANES), f32),
+        ],
+        compiler_params=pltpu.CompilerParams(vmem_limit_bytes=46 << 20),
+        cost_estimate=pl.CostEstimate(
+            flops=2 * inputs * STEPS * cells_all * LANES * 12, bytes_accessed=6 << 20, transcendentals=0
+        ),
+        name="main",
+    )(bounds, arranged, cells, levels)
     direct, adjoint, gram = pl.pallas_call(
-        functools.partial(window_kernel, inputs, width_x, depth_y),
+        functools.partial(rim_kernel, inputs, width_x, depth_y),
         out_shape=(
             jax.ShapeDtypeStruct((pair_count, 2 * inputs, 2 * LANES), jnp.bfloat16),
             jax.ShapeDtypeStruct((pair_count, 2 * inputs, 2 * LANES), jnp.bfloat16),
             jax.ShapeDtypeStruct((inputs, inputs), f32),
         ),
-        in_specs=[SMEM, SMEM] + [VMEM] * 6,
+        in_specs=[SMEM, SMEM] + [VMEM] * 5,
         out_specs=(VMEM, VMEM, VMEM),
         scratch_shapes=[
-            pltpu.VMEM((2, extent, rims * SUB, LANES), f32),
-            pltpu.VMEM((2, 4, extent, depth_y, SUB, LANES), f32),
-            pltpu.VMEM((groups + rims, extent, depth_y + 4, SUB, LANES), f32),
-            pltpu.VMEM((groups + rims, extent, depth_y + 4, SUB, LANES), f32),
-            pltpu.VMEM((2, width_x, depth_y, groups + rims, SUB, LANES), f32),
+            pltpu.VMEM((2 * rims, extent, SUB, LANES), f32),
+            pltpu.VMEM((4, extent, depth_y, SUB, LANES), f32),
+            pltpu.VMEM((2 * rims, extent, depth_y + 2 * PAD, SUB, LANES), f32),
+            pltpu.VMEM((2 * rims, extent, depth_y + 2 * PAD, SUB, LANES), f32),
+            pltpu.VMEM((2 * rims, width_x, depth_y, SUB, LANES), f32),
             pltpu.VMEM((3 * inputs, 3 * inputs), f32),
         ],
-        compiler_params=pltpu.CompilerParams(vmem_limit_bytes=34 << 20),
-        name="window",
-    )(bounds, flags, arranged, cells, rim, from_right, from_left, levels)
+        compiler_params=pltpu.CompilerParams(vmem_limit_bytes=22 << 20),
+        name="rim",
+    )(bounds, flags, rim, from_right, from_left, levels, field)
 
     gram = everywhere(gram, wide, narrow)
 
@@ -547,12 +623,12 @@
     direct_modes, adjoint_modes = pl.pallas_call(
         functools.partial(modes_kernel, inputs, width_x, depth_y, scale),
         out_shape=(shape, shape),
-        in_specs=[SMEM] + [VMEM] * 4,
-        out_specs=(VMEM, VMEM),
-        scratch_shapes=[pltpu.VMEM((inputs, rank_count), f32)],
+        in_specs=[VMEM] * 5,
+        out_specs=(pl.BlockSpec(memory_space=pltpu.HBM), VMEM),
+        scratch_shapes=[pltpu.VMEM(shape.shape, f32), pltpu.SemaphoreType.DMA],
         compiler_params=pltpu.CompilerParams(vmem_limit_bytes=7 << 20),
         name="modes",
-    )(ranks, gram, start_block, direct, adjoint)
+    )(ranks, gram, start_block.T, direct, adjoint)
     full = (rank_count, width_x, depth_y, width_z)
     return (direct_modes.reshape(full), adjoint_modes.reshape(full))
 

time: 85.3 us -> 73.8 us (0.87)
  waiting for transfers between devices: 14.1 us -> 9.07 us
  Pallas kernels: 42.3 us -> 38.4 us
  local copies, waits for them, and re-layouts: 5.02 us -> 2 us
    ppermute x1, waiting for transfers between devices: 5.13 us -> 0.01 us  [on_device(): from_right = lax.ppermute(rim, 'narrow', [(0, 1), (1, 0)])]
    pallas_call x1 -> x2, Pallas kernels: 30.9 us -> 27.5 us  [the longest x1 15.2 us: on_device(): pl.pallas_call(functools.partial(main_kernel, inputs, width_x, depth_y),...]
    unnamed x11 -> x6, local copies, waits for them, and re-layouts: 4.01 us -> 1 us
  transfers between devices with their start and end apart: 10 -> 10, of which waited for: 8 -> 7; matrix products, arithmetic and copies ran while one was open for 6% -> 6% of each run, Pallas kernels for 0% -> 21%
where the time goes in v2:
time: 73.8 us; the launch traced here: 73.6 us
  Pallas kernels  38.4 us (52%)
  starting transfers between devices  19.7 us (27%)
  waiting for transfers between devices  9.07 us (12%)
  other arithmetic  3.68 us (5%)
  local copies, waits for them, and re-layouts  2 us (3%)
  between operations  0.78 us (1%)
    pallas_call x1, Pallas kernels, on_device(): pl.pallas_call(functools.partial(main_kernel, inputs, width_x, depth_y),...  15.2 us
    ppermute x7, starting transfers between devices, other(): return lax.ppermute(value, axes, [(i, i ^ bit) for i in range(count)])  13 us
    pallas_call x1, Pallas kernels, on_device(): pl.pallas_call(functools.partial(rim_kernel, inputs, width_x, depth_y), o...  12.3 us
    ppermute x7, waiting for transfers between devices, other(): return lax.ppermute(value, axes, [(i, i ^ bit) for i in range(count)])  9.06 us
    pallas_call x1, Pallas kernels, on_device(): pl.pallas_call(functools.partial(modes_kernel, inputs, width_x, depth_y,...  6.96 us
    ppermute x1, starting transfers between devices, on_device(): near = lax.ppermute(sent, 'wide', near_pairs)  4.37 us
    pallas_call x1, Pallas kernels, on_device(): pl.pallas_call(functools.partial(pack_kernel, inputs, width_x, depth_y),...  2.15 us
    reduce_sum x2, other arithmetic, ordering(): rank = jnp.sum(ahead.astype(jnp.int32), axis=1)  1.83 us
  transfers between devices with their start and end apart: 10, of which 7 were waited for; matrix products, arithmetic and copies ran while one was open for 6% of the time, Pallas kernels for 21%

profile of v2, /device:TPU:0, one launch (start us, length us, event | category | flops | bytes accessed | tf_op | source)
XLA Modules:
  0.0 73.6 jit_solution(775875176189279439)
XLA Ops:
  0.6 1.8 %stage.1.here = f32[704,128]{1,0:T(8,128)} custom-call(f32[256,128]{1,0:T(8,128)} %bitcast.19, f32[256,128]{1,0:T(8,128)} %bitcast.20, f32[64,128]{1,0:T(8,128)} %bitcast.21, f32[64,128]{1,0:T(8,128)} %bitcast.22, f32[64,128]{1,0:T(8,128)} %bitcast.23), custom_call_target="tpu_custom_call" | custom-call | tf_op jit(solution)/shard_map/stage/pallas_call | solution.py:521
  2.4 0.7 collective-permute-start.1
  3.1 4.4 %collective-permute-start = (f32[704,128]{1,0:T(8,128)}, f32[704,128]{1,0:T(8,128)S(1)}, u32[]{:S(2)}, u32[]{:S(2)}) collective-permute-start(f32[704,128]{1,0:T(8,128)} %stage.1.here), channel_id=1, source_target_pairs={{0,2},{2,0},{4,6},{6,4},{8,10},{10,8},{12,14},{14,12},{16,18},{18,... | collective-permute-start | bytes 1081352 | tf_op jit(solution)/shard_map/ppermute | solution.py:531
  7.5 0.9 %convert_reduce_fusion = s32[64]{0:T(128)S(1)} fusion(s32[64]{0:T(128)} %param.14), kind=kLoop, calls=%fused_computation.7 | loop fusion | flops 28608 | bytes 512 | tf_op jit(solution)/shard_map/reduce_sum | solution.py:465
  8.4 0.8 %select_reduce_fusion = s32[64]{0:T(128)S(1)} fusion(s32[64]{0:T(128)S(1)} %convert_reduce_fusion, s32[64]{0:T(128)} %param.14), kind=kLoop, calls=%fused_computation.3 | loop fusion | flops 12224 | bytes 768 | tf_op jit(solution)/shard_map/reduce_sum | solution.py:466
  9.1 0.1 stack.72
  9.2 0.1 stack.68
  9.3 0.9 %convert_reduce_fusion.1 = s32[64]{0:T(128)S(1)} fusion(s32[64]{0:T(128)} %param.13), kind=kLoop, calls=%fused_computation.8 | loop fusion | flops 28608 | bytes 512 | tf_op jit(solution)/shard_map/reduce_sum | solution.py:465
  10.2 0.8 %select_reduce_fusion.1 = s32[64]{0:T(128)S(1)} fusion(s32[64]{0:T(128)S(1)} %convert_reduce_fusion.1, s32[64]{0:T(128)} %param.13), kind=kLoop, calls=%fused_computation.5 | loop fusion | flops 12224 | bytes 768 | tf_op jit(solution)/shard_map/reduce_sum | solution.py:466
  11.0 0.1 stack.71
  11.1 0.1 stack.67
  11.2 0.1 fusion.5
  11.3 0.1 pad_add_fusion.3.place_ref
  11.4 0.1 stack.86
  11.5 0.1 stack.85
  11.6 0.1 fusion.4
  11.6 0.0 collective-permute-done.1.far
  11.6 0.0 collective-permute-done.near
  11.6 0.0 copy-start
  11.7 1.0 %copy-done = f32[704,128]{1,0:T(8,128)S(1)} copy-done((f32[704,128]{1,0:T(8,128)S(1)}, f32[704,128]{1,0:T(8,128)}, u32[]{:S(2)}) %copy-start) | copy-done | bytes 360472
  12.6 2.1 %pack.1 = (f32[2,12,64,128]{3,2,1,0:T(8,128)S(1)}, f32[3,12,16,128]{3,2,1,0:T(8,128)S(1)}, f32[72,8,128]{2,1,0:T(8,128)S(1)}) custom-call(s32[2]{0:T(128)S(1)} %pad_add_fusion.3.place_ref, s32[2,64]{1,0:T(2,128)S(1)} %pad_add_fusion.1.rank_ref, f32[704,128]{1,0:T(8,128)S(1)} %copy-done, f32[704,128]{1,0:T(8,128)S(1)} %collective-permute-done.near, ...), custom_call_target="tpu_custom_call" | custom-call | tf_op jit(solution)/shard_map/pack/pallas_call | solution.py:558
  14.8 1.6 %collective-permute-start.2 = (f32[72,8,128]{2,1,0:T(8,128)S(1)}, f32[72,8,128]{2,1,0:T(8,128)S(1)}, u32[]{:S(2)}, u32[]{:S(2)}) collective-permute-start(f32[72,8,128]{2,1,0:T(8,128)S(1)} %get-tuple-element.10.rim_ref), channel_id=1, source_target_pairs={{0,1},{1,0},{2,3},{3,2},{4,5},{5,4},{6,7},{7,6},{8,9},{9,8},{10,11... | collective-permute-start | bytes 884744 | tf_op jit(solution)/shard_map/ppermute | solution.py:572
  16.4 0.1 add_convert_fusion.flag_ref
  16.4 0.1 copy.21
  16.5 0.1 broadcast_in_dim.20
  16.6 0.1 reshape_reshape.3
  16.7 0.1 add_add_fusion.2.bounds_ref
  16.8 0.1 broadcast_in_dim.19
  16.9 15.2 %main.1.field = f32[2,4,16,8,8,128]{5,4,3,2,1,0:T(8,128)S(1)} custom-call(s32[2,10,2]{2,1,0:T(8,128)S(1)} %add_add_fusion.2.bounds_ref, f32[2,12,64,128]{3,2,1,0:T(8,128)S(1)} %get-tuple-element.11.sorted_ref, f32[3,12,16,128]{3,2,1,0:T(8,128)S(1)} %get-tuple-element.12.cell_ref, s32[2,80,128]{2,1,0:T(8,128)S(1)} %pad_add_fusion.level_ref), custom_call_target="tpu_custom_call" | custom-call | flops 150994944 | bytes 6291456 | tf_op jit(solution)/shard_map/main/pallas_call | solution.py:582
  32.2 0.0 copy-start.1
  32.2 0.0 collective-permute-done.2.from_right.from_left
  32.2 12.3 %rim.1 = (bf16[32,128,256]{2,1,0:T(8,128)(2,1)S(1)}, bf16[32,128,256]{2,1,0:T(8,128)(2,1)S(1)}, f32[64,64]{1,0:T(8,128)S(1)}) custom-call(s32[2,10,2]{2,1,0:T(8,128)S(1)} %add_add_fusion.2.bounds_ref, s32[2]{0:T(128)S(1)} %add_convert_fusion.flag_ref, f32[72,8,128]{2,1,0:T(8,128)S(1)} %get-tuple-element.10.rim_ref, ...), custom_call_target="tpu_custom_call" | custom-call | tf_op jit(solution)/shard_map/rim/pallas_call | solution.py:598
  44.5 4.0 %collective-permute-start.3 = (f32[64,64]{1,0:T(8,128)S(1)}, f32[64,64]{1,0:T(8,128)S(1)}, u32[]{:S(2)}, u32[]{:S(2)}) collective-permute-start(f32[64,64]{1,0:T(8,128)S(1)} %get-tuple-element.13), channel_id=1, source_target_pairs={{0,2},{1,3},{2,0},{3,1},{4,6},{5,7},{6,4},{7,5},{8,10},{9,11},{10,... | collective-permute-start | bytes 49160 | tf_op jit(solution)/shard_map/ppermute | solution.py:479
  48.5 0.9 %collective-permute-done.3 = f32[64,64]{1,0:T(8,128)S(1)} collective-permute-done((f32[64,64]{1,0:T(8,128)S(1)}, f32[64,64]{1,0:T(8,128)S(1)}, u32[]{:S(2)}, u32[]{:S(2)}) %collective-permute-start.3) | collective-permute-done | bytes 16416 | tf_op jit(solution)/shard_map/ppermute | solution.py:479
  49.4 3.9 %collective-permute-start.6 = (f32[64,64]{1,0:T(8,128)S(1)}, f32[64,64]{1,0:T(8,128)S(1)}, u32[]{:S(2)}, u32[]{:S(2)}) collective-permute-start(f32[64,64]{1,0:T(8,128)S(1)} %add.30), channel_id=1, source_target_pairs={{0,12},{1,13},{2,14},{3,15},{4,8},{5,9},{6,10},{7,11},{8,4},{9,5},... | collective-permute-start | bytes 49160 | tf_op jit(solution)/shard_map/ppermute | solution.py:479
  53.3 0.4 collective-permute-start.5
  53.8 0.2 collective-permute-start.4
  54.0 1.3 %collective-permute-done.6 = f32[64,64]{1,0:T(8,128)S(1)} collective-permute-done((f32[64,64]{1,0:T(8,128)S(1)}, f32[64,64]{1,0:T(8,128)S(1)}, u32[]{:S(2)}, u32[]{:S(2)}) %collective-permute-start.6) | collective-permute-done | bytes 16416 | tf_op jit(solution)/shard_map/ppermute | solution.py:479
  55.2 2.0 %collective-permute-done.5 = f32[64,64]{1,0:T(8,128)S(1)} collective-permute-done((f32[64,64]{1,0:T(8,128)S(1)}, f32[64,64]{1,0:T(8,128)S(1)}, u32[]{:S(2)}, u32[]{:S(2)}) %collective-permute-start.5) | collective-permute-done | bytes 16416 | tf_op jit(solution)/shard_map/ppermute | solution.py:479
  57.2 0.4 collective-permute-done.4
  57.7 2.6 %collective-permute-start.9 = (f32[64,64]{1,0:T(8,128)S(1)}, f32[64,64]{1,0:T(8,128)S(1)}, u32[]{:S(2)}, u32[]{:S(2)}) collective-permute-start(f32[64,64]{1,0:T(8,128)S(1)} %add_add_fusion.1), channel_id=1, source_target_pairs={{0,17},{1,16},{2,19},{3,18},{4,21},{5,20},{6,23},{7,22},{8,25},{9,... | collective-permute-start | bytes 49160 | tf_op jit(solution)/shard_map/ppermute | solution.py:479
  60.3 1.5 %collective-permute-start.8 = (f32[64,64]{1,0:T(8,128)S(1)}, f32[64,64]{1,0:T(8,128)S(1)}, u32[]{:S(2)}, u32[]{:S(2)}) collective-permute-start(f32[64,64]{1,0:T(8,128)S(1)} %add_add_fusion.1), channel_id=1, source_target_pairs={{0,1},{1,0},{2,3},{3,2},{4,5},{5,4},{6,7},{7,6},{8,9},{9,8},{10,11... | collective-permute-start | bytes 49160 | tf_op jit(solution)/shard_map/ppermute | solution.py:479
  61.8 0.3 collective-permute-start.7
  62.1 2.0 %collective-permute-done.9 = f32[64,64]{1,0:T(8,128)S(1)} collective-permute-done((f32[64,64]{1,0:T(8,128)S(1)}, f32[64,64]{1,0:T(8,128)S(1)}, u32[]{:S(2)}, u32[]{:S(2)}) %collective-permute-start.9) | collective-permute-done | bytes 16416 | tf_op jit(solution)/shard_map/ppermute | solution.py:479
  64.2 0.2 collective-permute-done.8
  64.4 2.3 %collective-permute-done.7 = f32[64,64]{1,0:T(8,128)S(1)} collective-permute-done((f32[64,64]{1,0:T(8,128)S(1)}, f32[64,64]{1,0:T(8,128)S(1)}, u32[]{:S(2)}, u32[]{:S(2)}) %collective-permute-start.7) | collective-permute-done | bytes 16416 | tf_op jit(solution)/shard_map/ppermute | solution.py:479
  66.6 0.0 copy-done.1
  66.6 7.0 %modes.1 = (f32[2048,128]{1,0:T(8,128)}, f32[2048,128]{1,0:T(8,128)}) custom-call(s32[2,64]{1,0:T(2,128)S(1)} %pad_add_fusion.1.rank_ref, f32[64,64]{1,0:T(8,128)S(1)} %add_add_fusion.gram_ref, f32[32,64]{1,0:T(8,128)S(1)} %bitcast.18, bf16[32,128,256]{2,1,0:T(8,128)(2,1)S(1)} %get-tuple-element.14.direct_ref, ...), custom_call_target="tpu_custom_call" | custom-call | tf_op jit(solution)/shard_map/modes/pallas_call | solution.py:623
  (11 shorter events, 0.1 us)
Async XLA Ops:
  2.4 9.2 %collective-permute-start.1 = (f32[704,128]{1,0:T(8,128)}, f32[704,128]{1,0:T(8,128)S(1)}, u32[]{:S(2)}, u32[]{:S(2)}) collective-permute-start(f32[704,128]{1,0:T(8,128)} %stage.1.here), channel_id=1, source_target_pairs={{2,4},{4,2},{6,8},{8,6},{10,12},{12,10},{14,16},{16,14},{18,20},{2... | collective-permute-start | bytes 1081352 | tf_op jit(solution)/shard_map/ppermute | solution.py:532
  3.1 8.6 %collective-permute-start = (f32[704,128]{1,0:T(8,128)}, f32[704,128]{1,0:T(8,128)S(1)}, u32[]{:S(2)}, u32[]{:S(2)}) collective-permute-start(f32[704,128]{1,0:T(8,128)} %stage.1.here), channel_id=1, source_target_pairs={{0,2},{2,0},{4,6},{6,4},{8,10},{10,8},{12,14},{14,12},{16,18},{18,... | collective-permute-start | bytes 1081352 | tf_op jit(solution)/shard_map/ppermute | solution.py:531
  11.6 1.0 %copy-start = (f32[704,128]{1,0:T(8,128)S(1)}, f32[704,128]{1,0:T(8,128)}, u32[]{:S(2)}) copy-start(f32[704,128]{1,0:T(8,128)} %stage.1.here) | copy-start | bytes 1081348
  14.8 17.4 %collective-permute-start.2 = (f32[72,8,128]{2,1,0:T(8,128)S(1)}, f32[72,8,128]{2,1,0:T(8,128)S(1)}, u32[]{:S(2)}, u32[]{:S(2)}) collective-permute-start(f32[72,8,128]{2,1,0:T(8,128)S(1)} %get-tuple-element.10.rim_ref), channel_id=1, source_target_pairs={{0,1},{1,0},{2,3},{3,2},{4,5},{5,4},{6,7},{7,6},{8,9},{9,8},{10,11... | collective-permute-start | bytes 884744 | tf_op jit(solution)/shard_map/ppermute | solution.py:572
  32.2 34.5 %copy-start.1 = (f32[64,32]{0,1:T(8,128)S(1)}, f32[64,32]{0,1:T(8,128)}, u32[]{:S(2)}) copy-start(f32[64,32]{0,1:T(8,128)} %param.15) | copy-start | bytes 24580
  44.5 4.9 %collective-permute-start.3 = (f32[64,64]{1,0:T(8,128)S(1)}, f32[64,64]{1,0:T(8,128)S(1)}, u32[]{:S(2)}, u32[]{:S(2)}) collective-permute-start(f32[64,64]{1,0:T(8,128)S(1)} %get-tuple-element.13), channel_id=1, source_target_pairs={{0,2},{1,3},{2,0},{3,1},{4,6},{5,7},{6,4},{7,5},{8,10},{9,11},{10,... | collective-permute-start | bytes 49160 | tf_op jit(solution)/shard_map/ppermute | solution.py:479
  49.4 5.8 %collective-permute-start.6 = (f32[64,64]{1,0:T(8,128)S(1)}, f32[64,64]{1,0:T(8,128)S(1)}, u32[]{:S(2)}, u32[]{:S(2)}) collective-permute-start(f32[64,64]{1,0:T(8,128)S(1)} %add.30), channel_id=1, source_target_pairs={{0,12},{1,13},{2,14},{3,15},{4,8},{5,9},{6,10},{7,11},{8,4},{9,5},... | collective-permute-start | bytes 49160 | tf_op jit(solution)/shard_map/ppermute | solution.py:479
  53.3 3.9 %collective-permute-start.5 = (f32[64,64]{1,0:T(8,128)S(1)}, f32[64,64]{1,0:T(8,128)S(1)}, u32[]{:S(2)}, u32[]{:S(2)}) collective-permute-start(f32[64,64]{1,0:T(8,128)S(1)} %add.30), channel_id=1, source_target_pairs={{0,8},{1,9},{2,10},{3,11},{4,12},{5,13},{6,14},{7,15},{8,0},{9,1},... | collective-permute-start | bytes 49160 | tf_op jit(solution)/shard_map/ppermute | solution.py:479
  53.8 3.9 %collective-permute-start.4 = (f32[64,64]{1,0:T(8,128)S(1)}, f32[64,64]{1,0:T(8,128)S(1)}, u32[]{:S(2)}, u32[]{:S(2)}) collective-permute-start(f32[64,64]{1,0:T(8,128)S(1)} %add.30), channel_id=1, source_target_pairs={{0,4},{1,5},{2,6},{3,7},{4,0},{5,1},{6,2},{7,3},{8,12},{9,13},{10,... | collective-permute-start | bytes 49160 | tf_op jit(solution)/shard_map/ppermute | solution.py:479
  57.7 6.5 %collective-permute-start.9 = (f32[64,64]{1,0:T(8,128)S(1)}, f32[64,64]{1,0:T(8,128)S(1)}, u32[]{:S(2)}, u32[]{:S(2)}) collective-permute-start(f32[64,64]{1,0:T(8,128)S(1)} %add_add_fusion.1), channel_id=1, source_target_pairs={{0,17},{1,16},{2,19},{3,18},{4,21},{5,20},{6,23},{7,22},{8,25},{9,... | collective-permute-start | bytes 49160 | tf_op jit(solution)/shard_map/ppermute | solution.py:479
  60.3 4.1 %collective-permute-start.8 = (f32[64,64]{1,0:T(8,128)S(1)}, f32[64,64]{1,0:T(8,128)S(1)}, u32[]{:S(2)}, u32[]{:S(2)}) collective-permute-start(f32[64,64]{1,0:T(8,128)S(1)} %add_add_fusion.1), channel_id=1, source_target_pairs={{0,1},{1,0},{2,3},{3,2},{4,5},{5,4},{6,7},{7,6},{8,9},{9,8},{10,11... | collective-permute-start | bytes 49160 | tf_op jit(solution)/shard_map/ppermute | solution.py:479
  61.8 4.8 %collective-permute-start.7 = (f32[64,64]{1,0:T(8,128)S(1)}, f32[64,64]{1,0:T(8,128)S(1)}, u32[]{:S(2)}, u32[]{:S(2)}) collective-permute-start(f32[64,64]{1,0:T(8,128)S(1)} %add_add_fusion.1), channel_id=1, source_target_pairs={{0,16},{1,17},{2,18},{3,19},{4,20},{5,21},{6,22},{7,23},{8,24},{9,... | collective-permute-start | bytes 49160 | tf_op jit(solution)/shard_map/ppermute | solution.py:479

commit v3 on v2

--- a/solution.py
+++ b/solution.py
@@ -60,13 +60,26 @@
         copy.wait()
 
 
-def pack_kernel(
-    inputs, width_x, depth_y, place_ref, rank_ref, here, near, far,
-    sorted_ref, cell_ref, rim_ref,
-):
-    own = width_x
-    near_x = place_ref[0]
-    far_x = place_ref[1]
+def rim_row(inputs, depth_y, sorted_ref, cell_ref, at):
+    rims = inputs // SUB // PER
+    values = []
+    for system in range(2):
+        for rim in range(rims):
+            total = jnp.zeros((SUB, LANES), jnp.float32)
+            for slot in range(PER):
+                group = rim * PER + slot
+                total = total + edges(sorted_ref[system, at, group * SUB : (group + 1) * SUB, :], slot)
+            values.append(total)
+    pieces = [(which, tile) for which in range(3) for tile in range(depth_y // SUB)]
+    for first in range(0, len(pieces), PER):
+        total = jnp.zeros((SUB, LANES), jnp.float32)
+        for slot, (which, tile) in enumerate(pieces[first : first + PER]):
+            total = total + edges(cell_ref[which, at, tile * SUB : (tile + 1) * SUB, :], slot)
+        values.append(total)
+    return values
+
+
+def sort_rows(inputs, width_x, depth_y, rank_ref, sources, sorted_ref, cell_ref):
     for system in range(2):
         base = system * inputs * width_x
 
@@ -74,41 +87,39 @@
             to = rank_ref[system, j]
             for x in range(width_x):
                 row = base + j * width_x + x
-                sorted_ref[system, own + x, pl.ds(to, 1), :] = here[pl.ds(row, 1), :]
-                sorted_ref[system, near_x + x, pl.ds(to, 1), :] = near[pl.ds(row, 1), :]
-                sorted_ref[system, far_x + x, pl.ds(to, 1), :] = far[pl.ds(row, 1), :]
+                for first, source in sources:
+                    sorted_ref[system, first + x, pl.ds(to, 1), :] = source[pl.ds(row, 1), :]
             return carry
 
-        lax.fori_loop(0, inputs, move, 0, unroll=4)
+        lax.fori_loop(0, inputs, move, 0, unroll=8)
     start = 2 * inputs * width_x
     for which in range(3):
         for x in range(width_x):
             rows = pl.ds(start + (which * width_x + x) * depth_y, depth_y)
-            cell_ref[which, own + x] = here[rows, :]
-            cell_ref[which, near_x + x] = near[rows, :]
-            cell_ref[which, far_x + x] = far[rows, :]
-    groups = inputs // SUB
-    rims = groups // PER
+            for first, source in sources:
+                cell_ref[which, first + x] = source[rows, :]
+
+
+def own_kernel(inputs, width_x, depth_y, rank_ref, here, sorted_ref, cell_ref, rim_ref):
+    sort_rows(inputs, width_x, depth_y, rank_ref, [(0, here)], sorted_ref, cell_ref)
+    for x in range(width_x):
+        for index, value in enumerate(rim_row(inputs, depth_y, sorted_ref, cell_ref, x)):
+            rim_ref[index * width_x + x] = value
+
+
+def pack_kernel(
+    inputs, width_x, depth_y, place_ref, rank_ref, near, far, own_rim, sorted_ref, cell_ref, rim_ref
+):
+    sources = [(place_ref[0], near), (place_ref[1], far)]
+    sort_rows(inputs, width_x, depth_y, rank_ref, sources, sorted_ref, cell_ref)
     extent = 3 * width_x
-    tiles = depth_y // SUB
-
-    def rim_row(x, carry):
-        for system in range(2):
-            for rim in range(rims):
-                total = jnp.zeros((SUB, LANES), jnp.float32)
-                for slot in range(PER):
-                    group = rim * PER + slot
-                    total = total + edges(sorted_ref[system, x, group * SUB : (group + 1) * SUB, :], slot)
-                rim_ref[(system * rims + rim) * extent + x] = total
-        pieces = [(which, tile) for which in range(3) for tile in range(tiles)]
-        for at in range(0, len(pieces), PER):
-            total = jnp.zeros((SUB, LANES), jnp.float32)
-            for slot, (which, tile) in enumerate(pieces[at : at + PER]):
-                total = total + edges(cell_ref[which, x, tile * SUB : (tile + 1) * SUB, :], slot)
-            rim_ref[(2 * rims + at // PER) * extent + x] = total
-        return carry
-
-    lax.fori_loop(0, extent, rim_row, 0, unroll=extent)
+    for at in range(2 * width_x):
+        x = at if at < width_x else at + width_x
+        for index, value in enumerate(rim_row(inputs, depth_y, sorted_ref, cell_ref, at)):
+            rim_ref[index * extent + x] = value
+    for index in range(own_rim.shape[0] // width_x):
+        for x in range(width_x):
+            rim_ref[index * extent + width_x + x] = own_rim[index * width_x + x]
 
 
 def split(value):
@@ -133,23 +144,25 @@
     high0 = [bounds[system, row, 1] for system, row in units]
     top = depth_y - 1
 
-    for at in range(count):
-        levels = heights(at)
-        for x in range(extent):
-            for buffer in (ping, pong):
-                buffer[at, x, PAD - 1] = zero
-                buffer[at, x, PAD + depth_y] = zero
-
-        def begin(y, carry, at=at, levels=levels):
-            here = levels == y
+    def begin(trip, carry):
+        for at in range(count):
+            y = jnp.minimum(low0[at] + trip, high0[at])
+            here = heights(at) == y
             for x in range(extent):
                 value = jnp.where(here, load(at, x), 0.0)
                 if units[at][0]:
                     value = value * coef[1, x, y]
                 ping[at, x, y + PAD] = value
-            return carry
-
-        lax.fori_loop(low0[at], high0[at] + 1, begin, 0)
+        return carry
+
+    most = functools.reduce(jnp.maximum, [high0[at] - low0[at] + 1 for at in range(count)])
+    lax.fori_loop(0, most, begin, 0)
+    for at in range(count):
+        for x in range(extent):
+            for buffer in (ping, pong):
+                buffer[at, x, PAD - 1] = zero
+                buffer[at, x, PAD + depth_y] = zero
+
         for x in range(1, extent - 1):
             ping[at, x, low0[at] - 1 + PAD] = zero
             ping[at, x, high0[at] + 1 + PAD] = zero
@@ -231,18 +244,22 @@
 
 
 def main_kernel(
-    inputs, width_x, depth_y, bounds_ref, sorted_ref, cell_ref, level_ref, field, coef, ping, pong
+    inputs, width_x, depth_y, bounds_ref,
+    own_sorted, own_cells, sorted_ref, cell_ref, level_ref, field, coef, ping, pong,
 ):
     groups = inputs // SUB
     extent = 3 * width_x
 
-    def prepare(x, carry):
+    def place(x, own, halo):
+        if width_x <= x < 2 * width_x:
+            return own, x - width_x
+        return halo, x if x < width_x else x - width_x
+
+    for x in range(extent):
+        cells, at = place(x, own_cells, cell_ref)
         for tile in range(depth_y // SUB):
             rows = slice(tile * SUB, (tile + 1) * SUB)
-            store_cells(coef, x, tile, *(cell_ref[which, x, rows, :] for which in range(3)))
-        return carry
-
-    lax.fori_loop(0, extent, prepare, 0, unroll=2)
+            store_cells(coef, x, tile, *(cells[which, at, rows, :] for which in range(3)))
     units = [(system, group) for system in range(2) for group in range(groups)]
 
     def rows(at):
@@ -255,9 +272,13 @@
         for x in range(width_x):
             write(at, x, y, zero)
 
+    def load(at, x):
+        source, index = place(x, own_sorted, sorted_ref)
+        return source[units[at][0], index, rows(at), :]
+
     march(
         units, 1, depth_y, extent, bounds_ref,
-        lambda at, x: sorted_ref[units[at][0], x, rows(at), :],
+        load,
         lambda at: level_ref[units[at][0], rows(at), :],
         coef, ping, pong, write, wipe,
     )
@@ -359,9 +380,10 @@
     def part(row, column):
         return total_ref[row * inputs : (row + 1) * inputs, column * inputs : (column + 1) * inputs]
 
-    gram_ref[...] = (
+    gram = (
         (part(0, 2) + part(2, 0)) + part(1, 1) + (part(0, 1) + part(1, 0)) + part(0, 0)
     )
+    gram_ref[...] = jnp.concatenate([gram[: inputs // 2], gram[inputs // 2 :]], axis=1)
 
 
 def eliminate(matrix):
@@ -417,7 +439,7 @@
     ids = lax.broadcasted_iota(jnp.int32, (inputs, inputs), 0)
     chosen = jnp.where(rank_ref[0:1, :] == ids, 1.0, 0.0)
     start_sorted = product(chosen, start_ref[...], ((1,), (1,)))
-    gram = gram_ref[...] * scale
+    gram = jnp.concatenate([gram_ref[:, :inputs], gram_ref[:, inputs:]], axis=0) * scale
 
     def orthonormal(block):
         lower, pivots = eliminate(product(block, block, ((0,), (0,))))
@@ -553,20 +575,33 @@
     )
 
     odd = lax.axis_index("wide") % 2
-    place = jnp.stack([2 * width_x * (1 - odd), 2 * width_x * odd])
-    rim_count = (2 * rims + -(-3 * tiles // PER)) * extent
+    place = jnp.stack([width_x * (1 - odd), width_x * odd])
+    rim_kinds = 2 * rims + -(-3 * tiles // PER)
+    own_sorted, own_cells, own_rim = pl.pallas_call(
+        functools.partial(own_kernel, inputs, width_x, depth_y),
+        out_shape=(
+            jax.ShapeDtypeStruct((2, width_x, inputs, LANES), f32),
+            jax.ShapeDtypeStruct((3, width_x, depth_y, LANES), f32),
+            jax.ShapeDtypeStruct((rim_kinds * width_x, SUB, LANES), f32),
+        ),
+        in_specs=[SMEM, VMEM],
+        out_specs=(VMEM, VMEM, VMEM),
+        compiler_params=pltpu.CompilerParams(vmem_limit_bytes=8 << 20),
+        cost_estimate=pl.CostEstimate(flops=1 << 22, bytes_accessed=1 << 20, transcendentals=0),
+        name="own",
+    )(ranks, sent)
     arranged, cells, rim = pl.pallas_call(
         functools.partial(pack_kernel, inputs, width_x, depth_y),
         out_shape=(
-            jax.ShapeDtypeStruct((2, extent, inputs, LANES), f32),
-            jax.ShapeDtypeStruct((3, extent, depth_y, LANES), f32),
-            jax.ShapeDtypeStruct((rim_count, SUB, LANES), f32),
+            jax.ShapeDtypeStruct((2, 2 * width_x, inputs, LANES), f32),
+            jax.ShapeDtypeStruct((3, 2 * width_x, depth_y, LANES), f32),
+            jax.ShapeDtypeStruct((rim_kinds * extent, SUB, LANES), f32),
         ),
         in_specs=[SMEM, SMEM] + [VMEM] * 3,
         out_specs=(VMEM, VMEM, VMEM),
         compiler_params=pltpu.CompilerParams(vmem_limit_bytes=8 << 20),
         name="pack",
-    )(place, ranks, sent, near, far)
+    )(place, ranks, near, far, own_rim)
 
     if narrow == 2:
         from_right = lax.ppermute(rim, "narrow", [(0, 1), (1, 0)])
@@ -582,7 +617,7 @@
     field = pl.pallas_call(
         functools.partial(main_kernel, inputs, width_x, depth_y),
         out_shape=jax.ShapeDtypeStruct((2, width_x, depth_y, groups, SUB, LANES), f32),
-        in_specs=[SMEM] + [VMEM] * 3,
+        in_specs=[SMEM] + [VMEM] * 5,
         out_specs=VMEM,
         scratch_shapes=[
             pltpu.VMEM((4, extent, depth_y, SUB, LANES), f32),
@@ -594,13 +629,13 @@
             flops=2 * inputs * STEPS * cells_all * LANES * 12, bytes_accessed=6 << 20, transcendentals=0
         ),
         name="main",
-    )(bounds, arranged, cells, levels)
+    )(bounds, own_sorted, own_cells, arranged, cells, levels)
     direct, adjoint, gram = pl.pallas_call(
         functools.partial(rim_kernel, inputs, width_x, depth_y),
         out_shape=(
             jax.ShapeDtypeStruct((pair_count, 2 * inputs, 2 * LANES), jnp.bfloat16),
             jax.ShapeDtypeStruct((pair_count, 2 * inputs, 2 * LANES), jnp.bfloat16),
-            jax.ShapeDtypeStruct((inputs, inputs), f32),
+            jax.ShapeDtypeStruct((inputs // 2, 2 * inputs), f32),
         ),
         in_specs=[SMEM, SMEM] + [VMEM] * 5,
         out_specs=(VMEM, VMEM, VMEM),

time: 73.8 us -> 72.1 us (0.977)
  starting transfers between devices: 19.7 us -> 17.5 us
  Pallas kernels: 38.4 us -> 39.2 us
    ppermute x7, starting transfers between devices: 13 us -> 10.9 us  [other(): return lax.ppermute(value, axes, [(i, i ^ bit) for i in range(count)])]
    pallas_call x0 -> x1, Pallas kernels: none -> 1.12 us  [on_device(): pl.pallas_call(functools.partial(own_kernel, inputs, width_x, depth_y), o...]
  transfers between devices with their start and end apart: 10 -> 10, of which waited for: 7 -> 7; matrix products, arithmetic and copies ran while one was open for 6% -> 6% of each run, Pallas kernels for 21% -> 23%
where the time goes in v3:
time: 72.1 us; the launch traced here: 71.9 us
  Pallas kernels  39.2 us (54%)
  starting transfers between devices  17.5 us (24%)
  waiting for transfers between devices  8.7 us (12%)
  other arithmetic  3.67 us (5%)
  local copies, waits for them, and re-layouts  2 us (3%)
  between operations  0.77 us (1%)
    pallas_call x1, Pallas kernels, on_device(): pl.pallas_call(functools.partial(main_kernel, inputs, width_x, depth_y),...  15.4 us
    pallas_call x1, Pallas kernels, on_device(): pl.pallas_call(functools.partial(rim_kernel, inputs, width_x, depth_y), o...  12.4 us
    ppermute x7, starting transfers between devices, other(): return lax.ppermute(value, axes, [(i, i ^ bit) for i in range(count)])  10.9 us
    ppermute x7, waiting for transfers between devices, other(): return lax.ppermute(value, axes, [(i, i ^ bit) for i in range(count)])  8.69 us
    pallas_call x1, Pallas kernels, on_device(): pl.pallas_call(functools.partial(modes_kernel, inputs, width_x, depth_y,...  6.95 us
    ppermute x1, starting transfers between devices, on_device(): near = lax.ppermute(sent, 'wide', near_pairs)  4.37 us
    reduce_sum x2, other arithmetic, ordering(): rank = jnp.sum(ahead.astype(jnp.int32), axis=1)  1.83 us
    pallas_call x1, Pallas kernels, on_device(): pl.pallas_call(stage_kernel, out_shape=jax.ShapeDtypeStruct((sum((piece.s...  1.75 us
  transfers between devices with their start and end apart: 10, of which 7 were waited for; matrix products, arithmetic and copies ran while one was open for 6% of the time, Pallas kernels for 23%

profile of v3, /device:TPU:0, one launch (start us, length us, event | category | flops | bytes accessed | tf_op | source)
XLA Modules:
  0.0 71.9 jit_solution(12526482788852786406)
XLA Ops:
  0.6 1.8 %stage.1.here = f32[704,128]{1,0:T(8,128)} custom-call(f32[256,128]{1,0:T(8,128)} %bitcast.19, f32[256,128]{1,0:T(8,128)} %bitcast.20, f32[64,128]{1,0:T(8,128)} %bitcast.21, f32[64,128]{1,0:T(8,128)} %bitcast.22, f32[64,128]{1,0:T(8,128)} %bitcast.23), custom_call_target="tpu_custom_call" | custom-call | tf_op jit(solution)/shard_map/stage/pallas_call | solution.py:543
  2.4 0.7 collective-permute-start.1
  3.1 4.4 %collective-permute-start = (f32[704,128]{1,0:T(8,128)}, f32[704,128]{1,0:T(8,128)S(1)}, u32[]{:S(2)}, u32[]{:S(2)}) collective-permute-start(f32[704,128]{1,0:T(8,128)} %stage.1.here), channel_id=1, source_target_pairs={{0,2},{2,0},{4,6},{6,4},{8,10},{10,8},{12,14},{14,12},{16,18},{18,... | collective-permute-start | bytes 1081352 | tf_op jit(solution)/shard_map/ppermute | solution.py:553
  7.5 0.9 %convert_reduce_fusion = s32[64]{0:T(128)S(1)} fusion(s32[64]{0:T(128)} %param.14), kind=kLoop, calls=%fused_computation.5 | loop fusion | flops 28608 | bytes 512 | tf_op jit(solution)/shard_map/reduce_sum | solution.py:487
  8.4 0.8 %select_reduce_fusion = s32[64]{0:T(128)S(1)} fusion(s32[64]{0:T(128)S(1)} %convert_reduce_fusion, s32[64]{0:T(128)} %param.14), kind=kLoop, calls=%fused_computation.1 | loop fusion | flops 12224 | bytes 768 | tf_op jit(solution)/shard_map/reduce_sum | solution.py:488
  9.1 0.1 stack.72
  9.2 0.1 stack.68
  9.3 0.9 %convert_reduce_fusion.1 = s32[64]{0:T(128)S(1)} fusion(s32[64]{0:T(128)} %param.13), kind=kLoop, calls=%fused_computation.6 | loop fusion | flops 28608 | bytes 512 | tf_op jit(solution)/shard_map/reduce_sum | solution.py:487
  10.2 0.8 %select_reduce_fusion.1 = s32[64]{0:T(128)S(1)} fusion(s32[64]{0:T(128)S(1)} %convert_reduce_fusion.1, s32[64]{0:T(128)} %param.13), kind=kLoop, calls=%fused_computation.3 | loop fusion | flops 12224 | bytes 768 | tf_op jit(solution)/shard_map/reduce_sum | solution.py:488
  11.0 0.1 stack.71
  11.1 0.1 stack.67
  11.2 0.1 fusion.5
  11.3 0.1 pad_add_fusion.3.place_ref
  11.4 0.1 stack.86
  11.5 0.1 stack.85
  11.6 1.0 %copy-done = f32[704,128]{1,0:T(8,128)S(1)} copy-done((f32[704,128]{1,0:T(8,128)S(1)}, f32[704,128]{1,0:T(8,128)}, u32[]{:S(2)}) %copy-start) | copy-done | bytes 360472
  12.5 1.1 %own.1 = (f32[2,4,64,128]{3,2,1,0:T(8,128)S(1)}, f32[3,4,16,128]{3,2,1,0:T(8,128)S(1)}, f32[24,8,128]{2,1,0:T(8,128)S(1)}) custom-call(s32[2,64]{1,0:T(2,128)S(1)} %pad_add_fusion.1.rank_ref, f32[704,128]{1,0:T(8,128)S(1)} %copy-done), custom_call_target="tpu_custom_call" | custom-call | flops 4194304 | bytes 1048576 | tf_op jit(solution)/shard_map/own/pallas_call | solution.py:580
  13.7 0.1 fusion.4
  13.8 0.0 collective-permute-done.1.far
  13.8 0.0 collective-permute-done.near
  13.8 1.6 %pack.1 = (f32[2,8,64,128]{3,2,1,0:T(8,128)S(1)}, f32[3,8,16,128]{3,2,1,0:T(8,128)S(1)}, f32[72,8,128]{2,1,0:T(8,128)S(1)}) custom-call(s32[2]{0:T(128)S(1)} %pad_add_fusion.3.place_ref, s32[2,64]{1,0:T(2,128)S(1)} %pad_add_fusion.1.rank_ref, f32[704,128]{1,0:T(8,128)S(1)} %collective-permute-done.near, f32[704,128]{1,0:T(8,128)S(1)} %collective-permute-done.1.far, ...), custom_call_target="tpu_custom_call" | custom-call | tf_op jit(solution)/shard_map/pack/pallas_call | solution.py:593
  15.4 1.6 %collective-permute-start.2 = (f32[72,8,128]{2,1,0:T(8,128)S(1)}, f32[72,8,128]{2,1,0:T(8,128)S(1)}, u32[]{:S(2)}, u32[]{:S(2)}) collective-permute-start(f32[72,8,128]{2,1,0:T(8,128)S(1)} %get-tuple-element.14.rim_ref), channel_id=1, source_target_pairs={{0,1},{1,0},{2,3},{3,2},{4,5},{5,4},{6,7},{7,6},{8,9},{9,8},{10,11... | collective-permute-start | bytes 884744 | tf_op jit(solution)/shard_map/ppermute | solution.py:607
  17.0 0.1 add_convert_fusion.flag_ref
  17.1 0.1 copy.21
  17.2 0.1 broadcast_in_dim.20
  17.3 0.1 reshape_reshape.3
  17.4 0.1 add_add_fusion.bounds_ref
  17.4 0.1 broadcast_in_dim.19
  17.5 15.4 %main.1.field = f32[2,4,16,8,8,128]{5,4,3,2,1,0:T(8,128)S(1)} custom-call(s32[2,10,2]{2,1,0:T(8,128)S(1)} %add_add_fusion.bounds_ref, f32[2,4,64,128]{3,2,1,0:T(8,128)S(1)} %get-tuple-element.15.own_sorted, f32[3,4,16,128]{3,2,1,0:T(8,128)S(1)} %get-tuple-element.16.own_cells, f32[2,8,64,128]{3,2,1,0:T(8,128)S(1)} %get-tuple-element.17.sorted_ref, ...), custom_call_target="tpu_custom_call" | custom-call | flops 150994944 | bytes 6291456 | tf_op jit(solution)/shard_map/main/pallas_call | solution.py:617
  32.9 0.0 copy-start.1
  33.0 0.0 collective-permute-done.2.from_right.from_left
  33.0 12.4 %rim.1 = (bf16[32,128,256]{2,1,0:T(8,128)(2,1)S(1)}, bf16[32,128,256]{2,1,0:T(8,128)(2,1)S(1)}, f32[32,128]{1,0:T(8,128)S(1)}) custom-call(s32[2,10,2]{2,1,0:T(8,128)S(1)} %add_add_fusion.bounds_ref, s32[2]{0:T(128)S(1)} %add_convert_fusion.flag_ref, f32[72,8,128]{2,1,0:T(8,128)S(1)} %get-tuple-element.14.rim_ref, ...), custom_call_target="tpu_custom_call" | custom-call | tf_op jit(solution)/shard_map/rim/pallas_call | solution.py:633
  45.3 1.9 %collective-permute-start.3 = (f32[32,128]{1,0:T(8,128)S(1)}, f32[32,128]{1,0:T(8,128)S(1)}, u32[]{:S(2)}, u32[]{:S(2)}) collective-permute-start(f32[32,128]{1,0:T(8,128)S(1)} %get-tuple-element.19), channel_id=1, source_target_pairs={{0,2},{1,3},{2,0},{3,1},{4,6},{5,7},{6,4},{7,5},{8,10},{9,11},{10,... | collective-permute-start | bytes 49160 | tf_op jit(solution)/shard_map/ppermute | solution.py:501
  47.2 0.8 %collective-permute-done.3 = f32[32,128]{1,0:T(8,128)S(1)} collective-permute-done((f32[32,128]{1,0:T(8,128)S(1)}, f32[32,128]{1,0:T(8,128)S(1)}, u32[]{:S(2)}, u32[]{:S(2)}) %collective-permute-start.3) | collective-permute-done | bytes 16416 | tf_op jit(solution)/shard_map/ppermute | solution.py:501
  48.1 3.9 %collective-permute-start.6 = (f32[32,128]{1,0:T(8,128)S(1)}, f32[32,128]{1,0:T(8,128)S(1)}, u32[]{:S(2)}, u32[]{:S(2)}) collective-permute-start(f32[32,128]{1,0:T(8,128)S(1)} %add.30), channel_id=1, source_target_pairs={{0,12},{1,13},{2,14},{3,15},{4,8},{5,9},{6,10},{7,11},{8,4},{9,5},... | collective-permute-start | bytes 49160 | tf_op jit(solution)/shard_map/ppermute | solution.py:501
  52.0 0.4 collective-permute-start.5
  52.4 0.2 collective-permute-start.4
  52.6 1.1 %collective-permute-done.6 = f32[32,128]{1,0:T(8,128)S(1)} collective-permute-done((f32[32,128]{1,0:T(8,128)S(1)}, f32[32,128]{1,0:T(8,128)S(1)}, u32[]{:S(2)}, u32[]{:S(2)}) %collective-permute-start.6) | collective-permute-done | bytes 16416 | tf_op jit(solution)/shard_map/ppermute | solution.py:501
  53.7 2.0 %collective-permute-done.5 = f32[32,128]{1,0:T(8,128)S(1)} collective-permute-done((f32[32,128]{1,0:T(8,128)S(1)}, f32[32,128]{1,0:T(8,128)S(1)}, u32[]{:S(2)}, u32[]{:S(2)}) %collective-permute-start.5) | collective-permute-done | bytes 16416 | tf_op jit(solution)/shard_map/ppermute | solution.py:501
  55.7 0.4 collective-permute-done.4
  56.2 2.6 %collective-permute-start.9 = (f32[32,128]{1,0:T(8,128)S(1)}, f32[32,128]{1,0:T(8,128)S(1)}, u32[]{:S(2)}, u32[]{:S(2)}) collective-permute-start(f32[32,128]{1,0:T(8,128)S(1)} %add_add_fusion.2), channel_id=1, source_target_pairs={{0,17},{1,16},{2,19},{3,18},{4,21},{5,20},{6,23},{7,22},{8,25},{9,... | collective-permute-start | bytes 49160 | tf_op jit(solution)/shard_map/ppermute | solution.py:501
  58.8 1.5 %collective-permute-start.8 = (f32[32,128]{1,0:T(8,128)S(1)}, f32[32,128]{1,0:T(8,128)S(1)}, u32[]{:S(2)}, u32[]{:S(2)}) collective-permute-start(f32[32,128]{1,0:T(8,128)S(1)} %add_add_fusion.2), channel_id=1, source_target_pairs={{0,1},{1,0},{2,3},{3,2},{4,5},{5,4},{6,7},{7,6},{8,9},{9,8},{10,11... | collective-permute-start | bytes 49160 | tf_op jit(solution)/shard_map/ppermute | solution.py:501
  60.3 0.3 collective-permute-start.7
  60.6 1.4 %collective-permute-done.9 = f32[32,128]{1,0:T(8,128)S(1)} collective-permute-done((f32[32,128]{1,0:T(8,128)S(1)}, f32[32,128]{1,0:T(8,128)S(1)}, u32[]{:S(2)}, u32[]{:S(2)}) %collective-permute-start.9) | collective-permute-done | bytes 16416 | tf_op jit(solution)/shard_map/ppermute | solution.py:501
  62.0 0.5 collective-permute-done.8
  62.5 2.4 %collective-permute-done.7 = f32[32,128]{1,0:T(8,128)S(1)} collective-permute-done((f32[32,128]{1,0:T(8,128)S(1)}, f32[32,128]{1,0:T(8,128)S(1)}, u32[]{:S(2)}, u32[]{:S(2)}) %collective-permute-start.7) | collective-permute-done | bytes 16416 | tf_op jit(solution)/shard_map/ppermute | solution.py:501
  64.9 0.0 copy-done.1
  64.9 7.0 %modes.1 = (f32[2048,128]{1,0:T(8,128)}, f32[2048,128]{1,0:T(8,128)}) custom-call(s32[2,64]{1,0:T(2,128)S(1)} %pad_add_fusion.1.rank_ref, f32[32,128]{1,0:T(8,128)S(1)} %add_add_fusion.1.gram_ref, f32[32,64]{1,0:T(8,128)S(1)} %bitcast.18, bf16[32,128,256]{2,1,0:T(8,128)(2,1)S(1)} %get-tuple-element.20.direct_ref, ...), custom_call_target="tpu_custom_call" | custom-call | tf_op jit(solution)/shard_map/modes/pallas_call | solution.py:658
  (12 shorter events, 0.1 us)
Async XLA Ops:
  2.4 11.4 %collective-permute-start.1 = (f32[704,128]{1,0:T(8,128)}, f32[704,128]{1,0:T(8,128)S(1)}, u32[]{:S(2)}, u32[]{:S(2)}) collective-permute-start(f32[704,128]{1,0:T(8,128)} %stage.1.here), channel_id=1, source_target_pairs={{2,4},{4,2},{6,8},{8,6},{10,12},{12,10},{14,16},{16,14},{18,20},{2... | collective-permute-start | bytes 1081352 | tf_op jit(solution)/shard_map/ppermute | solution.py:554
  3.1 10.7 %collective-permute-start = (f32[704,128]{1,0:T(8,128)}, f32[704,128]{1,0:T(8,128)S(1)}, u32[]{:S(2)}, u32[]{:S(2)}) collective-permute-start(f32[704,128]{1,0:T(8,128)} %stage.1.here), channel_id=1, source_target_pairs={{0,2},{2,0},{4,6},{6,4},{8,10},{10,8},{12,14},{14,12},{16,18},{18,... | collective-permute-start | bytes 1081352 | tf_op jit(solution)/shard_map/ppermute | solution.py:553
  11.6 1.0 %copy-start = (f32[704,128]{1,0:T(8,128)S(1)}, f32[704,128]{1,0:T(8,128)}, u32[]{:S(2)}) copy-start(f32[704,128]{1,0:T(8,128)} %stage.1.here) | copy-start | bytes 1081348
  15.4 17.5 %collective-permute-start.2 = (f32[72,8,128]{2,1,0:T(8,128)S(1)}, f32[72,8,128]{2,1,0:T(8,128)S(1)}, u32[]{:S(2)}, u32[]{:S(2)}) collective-permute-start(f32[72,8,128]{2,1,0:T(8,128)S(1)} %get-tuple-element.14.rim_ref), channel_id=1, source_target_pairs={{0,1},{1,0},{2,3},{3,2},{4,5},{5,4},{6,7},{7,6},{8,9},{9,8},{10,11... | collective-permute-start | bytes 884744 | tf_op jit(solution)/shard_map/ppermute | solution.py:607
  32.9 32.0 %copy-start.1 = (f32[64,32]{0,1:T(8,128)S(1)}, f32[64,32]{0,1:T(8,128)}, u32[]{:S(2)}) copy-start(f32[64,32]{0,1:T(8,128)} %param.15) | copy-start | bytes 24580
  45.3 2.7 %collective-permute-start.3 = (f32[32,128]{1,0:T(8,128)S(1)}, f32[32,128]{1,0:T(8,128)S(1)}, u32[]{:S(2)}, u32[]{:S(2)}) collective-permute-start(f32[32,128]{1,0:T(8,128)S(1)} %get-tuple-element.19), channel_id=1, source_target_pairs={{0,2},{1,3},{2,0},{3,1},{4,6},{5,7},{6,4},{7,5},{8,10},{9,11},{10,... | collective-permute-start | bytes 49160 | tf_op jit(solution)/shard_map/ppermute | solution.py:501
  48.1 5.6 %collective-permute-start.6 = (f32[32,128]{1,0:T(8,128)S(1)}, f32[32,128]{1,0:T(8,128)S(1)}, u32[]{:S(2)}, u32[]{:S(2)}) collective-permute-start(f32[32,128]{1,0:T(8,128)S(1)} %add.30), channel_id=1, source_target_pairs={{0,12},{1,13},{2,14},{3,15},{4,8},{5,9},{6,10},{7,11},{8,4},{9,5},... | collective-permute-start | bytes 49160 | tf_op jit(solution)/shard_map/ppermute | solution.py:501
  52.0 3.7 %collective-permute-start.5 = (f32[32,128]{1,0:T(8,128)S(1)}, f32[32,128]{1,0:T(8,128)S(1)}, u32[]{:S(2)}, u32[]{:S(2)}) collective-permute-start(f32[32,128]{1,0:T(8,128)S(1)} %add.30), channel_id=1, source_target_pairs={{0,8},{1,9},{2,10},{3,11},{4,12},{5,13},{6,14},{7,15},{8,0},{9,1},... | collective-permute-start | bytes 49160 | tf_op jit(solution)/shard_map/ppermute | solution.py:501
  52.4 3.7 %collective-permute-start.4 = (f32[32,128]{1,0:T(8,128)S(1)}, f32[32,128]{1,0:T(8,128)S(1)}, u32[]{:S(2)}, u32[]{:S(2)}) collective-permute-start(f32[32,128]{1,0:T(8,128)S(1)} %add.30), channel_id=1, source_target_pairs={{0,4},{1,5},{2,6},{3,7},{4,0},{5,1},{6,2},{7,3},{8,12},{9,13},{10,... | collective-permute-start | bytes 49160 | tf_op jit(solution)/shard_map/ppermute | solution.py:501
  56.2 5.8 %collective-permute-start.9 = (f32[32,128]{1,0:T(8,128)S(1)}, f32[32,128]{1,0:T(8,128)S(1)}, u32[]{:S(2)}, u32[]{:S(2)}) collective-permute-start(f32[32,128]{1,0:T(8,128)S(1)} %add_add_fusion.2), channel_id=1, source_target_pairs={{0,17},{1,16},{2,19},{3,18},{4,21},{5,20},{6,23},{7,22},{8,25},{9,... | collective-permute-start | bytes 49160 | tf_op jit(solution)/shard_map/ppermute | solution.py:501
  58.8 3.7 %collective-permute-start.8 = (f32[32,128]{1,0:T(8,128)S(1)}, f32[32,128]{1,0:T(8,128)S(1)}, u32[]{:S(2)}, u32[]{:S(2)}) collective-permute-start(f32[32,128]{1,0:T(8,128)S(1)} %add_add_fusion.2), channel_id=1, source_target_pairs={{0,1},{1,0},{2,3},{3,2},{4,5},{5,4},{6,7},{7,6},{8,9},{9,8},{10,11... | collective-permute-start | bytes 49160 | tf_op jit(solution)/shard_map/ppermute | solution.py:501
  60.3 4.6 %collective-permute-start.7 = (f32[32,128]{1,0:T(8,128)S(1)}, f32[32,128]{1,0:T(8,128)S(1)}, u32[]{:S(2)}, u32[]{:S(2)}) collective-permute-start(f32[32,128]{1,0:T(8,128)S(1)} %add_add_fusion.2), channel_id=1, source_target_pairs={{0,16},{1,17},{2,18},{3,19},{4,20},{5,21},{6,22},{7,23},{8,24},{9,... | collective-permute-start | bytes 49160 | tf_op jit(solution)/shard_map/ppermute | solution.py:501

commit v4 on v3

--- a/solution.py
+++ b/solution.py
@@ -143,6 +143,8 @@
     low0 = [bounds[system, row, 0] for system, row in units]
     high0 = [bounds[system, row, 1] for system, row in units]
     top = depth_y - 1
+    per = count // 2
+    span = max(share, 1)
 
     def begin(trip, carry):
         for at in range(count):
@@ -172,11 +174,11 @@
         low = [jnp.maximum(bound - level + 1, 0) for bound in low0]
         high = [jnp.minimum(bound + level - 1, top) for bound in high0]
         trips = functools.reduce(
-            jnp.maximum, [(high[at] - low[at] + share) // share for at in range(count)]
+            jnp.maximum, [(high[at] - low[at] + span) // span for at in range(count)]
         )
 
-        def plane(at, y, level=level, source=source, target=target):
-            system = units[at][0]
+        def plane(system, row, y, level=level, source=source, target=target):
+            at = system * per + row
             rows = {}
             carried = {}
             for x in range(level - 1, extent - level + 1):
@@ -199,15 +201,39 @@
                 else:
                     value = coef[0, x, y] * here + coef[1, x, y] * total
                 if level == STEPS:
-                    write(at, x - level, y, value)
+                    write(system, row, x - level, y, value)
                 else:
                     target[at, x, y + PAD] = value
 
-        def step(trip, carry, low=low, high=high, plane=plane):
+        if share:
+
+            def step(trip, carry, low=low, high=high, plane=plane):
+                for at in range(count):
+                    for more in range(share):
+                        y = jnp.minimum(low[at] + (trip * share + more), high[at])
+                        plane(units[at][0], at % per, y)
+                return carry
+
+        else:
+            ends, bases = [], []
             for at in range(count):
-                for more in range(share):
-                    plane(at, jnp.minimum(low[at] + (trip * share + more), high[at]))
-            return carry
+                before = 0 if at % per == 0 else ends[-1]
+                bases.append(low[at] - before)
+                ends.append(before + high[at] - low[at] + 1)
+            trips = (jnp.maximum(ends[per - 1], ends[count - 1]) + per - 1) // per
+
+            def step(trip, carry, ends=ends, bases=bases, plane=plane):
+                for system in range(2):
+                    first = system * per
+                    for more in range(per):
+                        place = jnp.minimum(trip * per + more, ends[first + per - 1] - 1)
+                        row, base = 0, bases[first]
+                        for other in range(per - 1):
+                            later = place >= ends[first + other]
+                            row = jnp.where(later, other + 1, row)
+                            base = jnp.where(later, bases[first + other + 1], base)
+                        plane(system, row, place + base)
+                return carry
 
         lax.fori_loop(0, trips, step, 0)
         for at in range(count):
@@ -231,7 +257,7 @@
                             value = source[at, x, y + inner + PAD]
                             if not units[at][0]:
                                 value = coef[1, x, y] * value
-                            write(at, x - level, y, value)
+                            write(units[at][0], at % per, x - level, y, value)
 
             if level == STEPS:
 
@@ -265,19 +291,19 @@
     def rows(at):
         return slice(units[at][1] * SUB, (units[at][1] + 1) * SUB)
 
-    def write(at, x, y, value):
-        field[units[at][0], x, y, units[at][1]] = value
+    def write(system, row, x, y, value):
+        field[system, x, y, row] = value
 
     def wipe(at, y, zero):
         for x in range(width_x):
-            write(at, x, y, zero)
+            write(units[at][0], units[at][1], x, y, zero)
 
     def load(at, x):
         source, index = place(x, own_sorted, sorted_ref)
         return source[units[at][0], index, rows(at), :]
 
     march(
-        units, 1, depth_y, extent, bounds_ref,
+        units, 0, depth_y, extent, bounds_ref,
         load,
         lambda at: level_ref[units[at][0], rows(at), :],
         coef, ping, pong, write, wipe,
@@ -330,15 +356,15 @@
     def rows(at):
         return slice(units[at][1] * SUB, (units[at][1] + 1) * SUB)
 
-    def write(at, x, y, value):
-        edge_field[at, x, y] = value
+    def write(system, row, x, y, value):
+        edge_field[system * rims + row, x, y] = value
 
     def wipe(at, y, zero):
         for x in range(width_x):
-            write(at, x, y, zero)
+            edge_field[at, x, y] = zero
 
     march(
-        units, 2, depth_y, extent, bounds_ref,
+        units, 3, depth_y, extent, bounds_ref,
         lambda at, x: amp[at, x],
         lambda at: level_ref[units[at][0], rows(at), :],
         coef, ping, pong, write, wipe,
@@ -375,7 +401,7 @@
         )
         return carry
 
-    lax.fori_loop(0, width_x * pairs, fold, 0, unroll=4)
+    lax.fori_loop(0, width_x * pairs, fold, 0, unroll=8)
 
     def part(row, column):
         return total_ref[row * inputs : (row + 1) * inputs, column * inputs : (column + 1) * inputs]
@@ -471,7 +497,7 @@
                 ]
             return carry
 
-        lax.fori_loop(0, width_x * pairs, project, 0, unroll=8)
+        lax.fori_loop(0, width_x * pairs, project, 0, unroll=16)
         if out is direct_hold:
             leave = pltpu.make_async_copy(direct_hold, direct_out, sem)
             leave.start()

time: 72.1 us -> 67.9 us (0.942)
  Pallas kernels: 39.2 us -> 35 us
    pallas_call x1, Pallas kernels: 15.4 us -> 12.9 us  [on_device(): pl.pallas_call(functools.partial(main_kernel, inputs, width_x, depth_y),...]
    pallas_call x1, Pallas kernels: 12.4 us -> 11.1 us  [on_device(): pl.pallas_call(functools.partial(rim_kernel, inputs, width_x, depth_y), o...]
  transfers between devices with their start and end apart: 10 -> 10, of which waited for: 7 -> 7; matrix products, arithmetic and copies ran while one was open for 6% -> 7% of each run, Pallas kernels for 23% -> 21%
where the time goes in v4:
time: 67.9 us; the launch traced here: 67.7 us
  Pallas kernels  35 us (52%)
  starting transfers between devices  17.5 us (26%)
  waiting for transfers between devices  8.7 us (13%)
  other arithmetic  3.67 us (5%)
  local copies, waits for them, and re-layouts  2 us (3%)
  between operations  0.77 us (1%)
    pallas_call x1, Pallas kernels, on_device(): pl.pallas_call(functools.partial(main_kernel, inputs, width_x, depth_y),...  12.9 us
    pallas_call x1, Pallas kernels, on_device(): pl.pallas_call(functools.partial(rim_kernel, inputs, width_x, depth_y), o...  11.1 us
    ppermute x7, starting transfers between devices, other(): return lax.ppermute(value, axes, [(i, i ^ bit) for i in range(count)])  10.9 us
    ppermute x7, waiting for transfers between devices, other(): return lax.ppermute(value, axes, [(i, i ^ bit) for i in range(count)])  8.69 us
    pallas_call x1, Pallas kernels, on_device(): pl.pallas_call(functools.partial(modes_kernel, inputs, width_x, depth_y,...  6.54 us
    ppermute x1, starting transfers between devices, on_device(): near = lax.ppermute(sent, 'wide', near_pairs)  4.37 us
    reduce_sum x2, other arithmetic, ordering(): rank = jnp.sum(ahead.astype(jnp.int32), axis=1)  1.83 us
    pallas_call x1, Pallas kernels, on_device(): pl.pallas_call(stage_kernel, out_shape=jax.ShapeDtypeStruct((sum((piece.s...  1.75 us
  transfers between devices with their start and end apart: 10, of which 7 were waited for; matrix products, arithmetic and copies ran while one was open for 7% of the time, Pallas kernels for 21%

profile of v4, /device:TPU:0, one launch (start us, length us, event | category | flops | bytes accessed | tf_op | source)
XLA Modules:
  0.0 67.7 jit_solution(10674196621561372559)
XLA Ops:
  0.6 1.8 %stage.1.here = f32[704,128]{1,0:T(8,128)} custom-call(f32[256,128]{1,0:T(8,128)} %bitcast.19, f32[256,128]{1,0:T(8,128)} %bitcast.20, f32[64,128]{1,0:T(8,128)} %bitcast.21, f32[64,128]{1,0:T(8,128)} %bitcast.22, f32[64,128]{1,0:T(8,128)} %bitcast.23), custom_call_target="tpu_custom_call" | custom-call | tf_op jit(solution)/shard_map/stage/pallas_call | solution.py:569
  2.4 0.7 %collective-permute-start.1 = (f32[704,128]{1,0:T(8,128)}, f32[704,128]{1,0:T(8,128)S(1)}, u32[]{:S(2)}, u32[]{:S(2)}) collective-permute-start(f32[704,128]{1,0:T(8,128)} %stage.1.here), channel_id=1, source_target_pairs={{2,4},{4,2},{6,8},{8,6},{10,12},{12,10},{14,16},{16,14},{18,20},{2... | collective-permute-start | bytes 1081352 | tf_op jit(solution)/shard_map/ppermute | solution.py:580
  3.1 4.4 %collective-permute-start = (f32[704,128]{1,0:T(8,128)}, f32[704,128]{1,0:T(8,128)S(1)}, u32[]{:S(2)}, u32[]{:S(2)}) collective-permute-start(f32[704,128]{1,0:T(8,128)} %stage.1.here), channel_id=1, source_target_pairs={{0,2},{2,0},{4,6},{6,4},{8,10},{10,8},{12,14},{14,12},{16,18},{18,... | collective-permute-start | bytes 1081352 | tf_op jit(solution)/shard_map/ppermute | solution.py:579
  7.5 0.9 %convert_reduce_fusion = s32[64]{0:T(128)S(1)} fusion(s32[64]{0:T(128)} %param.14), kind=kLoop, calls=%fused_computation.5 | loop fusion | flops 28608 | bytes 512 | tf_op jit(solution)/shard_map/reduce_sum | solution.py:513
  8.4 0.8 %select_reduce_fusion = s32[64]{0:T(128)S(1)} fusion(s32[64]{0:T(128)S(1)} %convert_reduce_fusion, s32[64]{0:T(128)} %param.14), kind=kLoop, calls=%fused_computation.1 | loop fusion | flops 12224 | bytes 768 | tf_op jit(solution)/shard_map/reduce_sum | solution.py:514
  9.1 0.1 stack.72
  9.2 0.1 stack.68
  9.3 0.9 %convert_reduce_fusion.1 = s32[64]{0:T(128)S(1)} fusion(s32[64]{0:T(128)} %param.13), kind=kLoop, calls=%fused_computation.6 | loop fusion | flops 28608 | bytes 512 | tf_op jit(solution)/shard_map/reduce_sum | solution.py:513
  10.2 0.8 %select_reduce_fusion.1 = s32[64]{0:T(128)S(1)} fusion(s32[64]{0:T(128)S(1)} %convert_reduce_fusion.1, s32[64]{0:T(128)} %param.13), kind=kLoop, calls=%fused_computation.3 | loop fusion | flops 12224 | bytes 768 | tf_op jit(solution)/shard_map/reduce_sum | solution.py:514
  11.0 0.1 stack.71
  11.1 0.1 stack.67
  11.2 0.1 fusion.5
  11.3 0.1 pad_add_fusion.3.place_ref
  11.4 0.1 stack.86
  11.5 0.1 stack.85
  11.6 1.0 %copy-done = f32[704,128]{1,0:T(8,128)S(1)} copy-done((f32[704,128]{1,0:T(8,128)S(1)}, f32[704,128]{1,0:T(8,128)}, u32[]{:S(2)}) %copy-start) | copy-done | bytes 360472
  12.5 1.1 %own.1 = (f32[2,4,64,128]{3,2,1,0:T(8,128)S(1)}, f32[3,4,16,128]{3,2,1,0:T(8,128)S(1)}, f32[24,8,128]{2,1,0:T(8,128)S(1)}) custom-call(s32[2,64]{1,0:T(2,128)S(1)} %pad_add_fusion.1.rank_ref, f32[704,128]{1,0:T(8,128)S(1)} %copy-done), custom_call_target="tpu_custom_call" | custom-call | flops 4194304 | bytes 1048576 | tf_op jit(solution)/shard_map/own/pallas_call | solution.py:606
  13.7 0.1 fusion.4
  13.8 0.0 collective-permute-done.1.far
  13.8 0.0 collective-permute-done.near
  13.8 1.6 %pack.1 = (f32[2,8,64,128]{3,2,1,0:T(8,128)S(1)}, f32[3,8,16,128]{3,2,1,0:T(8,128)S(1)}, f32[72,8,128]{2,1,0:T(8,128)S(1)}) custom-call(s32[2]{0:T(128)S(1)} %pad_add_fusion.3.place_ref, s32[2,64]{1,0:T(2,128)S(1)} %pad_add_fusion.1.rank_ref, f32[704,128]{1,0:T(8,128)S(1)} %collective-permute-done.near, f32[704,128]{1,0:T(8,128)S(1)} %collective-permute-done.1.far, ...), custom_call_target="tpu_custom_call" | custom-call | tf_op jit(solution)/shard_map/pack/pallas_call | solution.py:619
  15.4 1.6 %collective-permute-start.2 = (f32[72,8,128]{2,1,0:T(8,128)S(1)}, f32[72,8,128]{2,1,0:T(8,128)S(1)}, u32[]{:S(2)}, u32[]{:S(2)}) collective-permute-start(f32[72,8,128]{2,1,0:T(8,128)S(1)} %get-tuple-element.14.rim_ref), channel_id=1, source_target_pairs={{0,1},{1,0},{2,3},{3,2},{4,5},{5,4},{6,7},{7,6},{8,9},{9,8},{10,11... | collective-permute-start | bytes 884744 | tf_op jit(solution)/shard_map/ppermute | solution.py:633
  17.0 0.1 add_convert_fusion.flag_ref
  17.1 0.1 copy.21
  17.2 0.1 broadcast_in_dim.20
  17.3 0.1 reshape_reshape.3
  17.4 0.1 add_add_fusion.bounds_ref
  17.4 0.1 broadcast_in_dim.19
  17.5 12.9 %main.1.field = f32[2,4,16,8,8,128]{5,4,3,2,1,0:T(8,128)S(1)} custom-call(s32[2,10,2]{2,1,0:T(8,128)S(1)} %add_add_fusion.bounds_ref, f32[2,4,64,128]{3,2,1,0:T(8,128)S(1)} %get-tuple-element.15.own_sorted, f32[3,4,16,128]{3,2,1,0:T(8,128)S(1)} %get-tuple-element.16.own_cells, f32[2,8,64,128]{3,2,1,0:T(8,128)S(1)} %get-tuple-element.17.sorted_ref, ...), custom_call_target="tpu_custom_call" | custom-call | flops 150994944 | bytes 6291456 | tf_op jit(solution)/shard_map/main/pallas_call | solution.py:643
  30.4 0.0 copy-start.1
  30.5 0.0 collective-permute-done.2.from_right.from_left
  30.5 11.1 %rim.1 = (bf16[32,128,256]{2,1,0:T(8,128)(2,1)S(1)}, bf16[32,128,256]{2,1,0:T(8,128)(2,1)S(1)}, f32[32,128]{1,0:T(8,128)S(1)}) custom-call(s32[2,10,2]{2,1,0:T(8,128)S(1)} %add_add_fusion.bounds_ref, s32[2]{0:T(128)S(1)} %add_convert_fusion.flag_ref, f32[72,8,128]{2,1,0:T(8,128)S(1)} %get-tuple-element.14.rim_ref, ...), custom_call_target="tpu_custom_call" | custom-call | tf_op jit(solution)/shard_map/rim/pallas_call | solution.py:659
  41.5 1.9 %collective-permute-start.3 = (f32[32,128]{1,0:T(8,128)S(1)}, f32[32,128]{1,0:T(8,128)S(1)}, u32[]{:S(2)}, u32[]{:S(2)}) collective-permute-start(f32[32,128]{1,0:T(8,128)S(1)} %get-tuple-element.19), channel_id=1, source_target_pairs={{0,2},{1,3},{2,0},{3,1},{4,6},{5,7},{6,4},{7,5},{8,10},{9,11},{10,... | collective-permute-start | bytes 49160 | tf_op jit(solution)/shard_map/ppermute | solution.py:527
  43.4 0.8 %collective-permute-done.3 = f32[32,128]{1,0:T(8,128)S(1)} collective-permute-done((f32[32,128]{1,0:T(8,128)S(1)}, f32[32,128]{1,0:T(8,128)S(1)}, u32[]{:S(2)}, u32[]{:S(2)}) %collective-permute-start.3) | collective-permute-done | bytes 16416 | tf_op jit(solution)/shard_map/ppermute | solution.py:527
  44.3 3.9 %collective-permute-start.6 = (f32[32,128]{1,0:T(8,128)S(1)}, f32[32,128]{1,0:T(8,128)S(1)}, u32[]{:S(2)}, u32[]{:S(2)}) collective-permute-start(f32[32,128]{1,0:T(8,128)S(1)} %add.30), channel_id=1, source_target_pairs={{0,12},{1,13},{2,14},{3,15},{4,8},{5,9},{6,10},{7,11},{8,4},{9,5},... | collective-permute-start | bytes 49160 | tf_op jit(solution)/shard_map/ppermute | solution.py:527
  48.2 0.4 collective-permute-start.5
  48.6 0.2 collective-permute-start.4
  48.8 1.1 %collective-permute-done.6 = f32[32,128]{1,0:T(8,128)S(1)} collective-permute-done((f32[32,128]{1,0:T(8,128)S(1)}, f32[32,128]{1,0:T(8,128)S(1)}, u32[]{:S(2)}, u32[]{:S(2)}) %collective-permute-start.6) | collective-permute-done | bytes 16416 | tf_op jit(solution)/shard_map/ppermute | solution.py:527
  49.9 2.0 %collective-permute-done.5 = f32[32,128]{1,0:T(8,128)S(1)} collective-permute-done((f32[32,128]{1,0:T(8,128)S(1)}, f32[32,128]{1,0:T(8,128)S(1)}, u32[]{:S(2)}, u32[]{:S(2)}) %collective-permute-start.5) | collective-permute-done | bytes 16416 | tf_op jit(solution)/shard_map/ppermute | solution.py:527
  51.9 0.4 collective-permute-done.4
  52.4 2.6 %collective-permute-start.9 = (f32[32,128]{1,0:T(8,128)S(1)}, f32[32,128]{1,0:T(8,128)S(1)}, u32[]{:S(2)}, u32[]{:S(2)}) collective-permute-start(f32[32,128]{1,0:T(8,128)S(1)} %add_add_fusion.2), channel_id=1, source_target_pairs={{0,17},{1,16},{2,19},{3,18},{4,21},{5,20},{6,23},{7,22},{8,25},{9,... | collective-permute-start | bytes 49160 | tf_op jit(solution)/shard_map/ppermute | solution.py:527
  55.0 1.5 %collective-permute-start.8 = (f32[32,128]{1,0:T(8,128)S(1)}, f32[32,128]{1,0:T(8,128)S(1)}, u32[]{:S(2)}, u32[]{:S(2)}) collective-permute-start(f32[32,128]{1,0:T(8,128)S(1)} %add_add_fusion.2), channel_id=1, source_target_pairs={{0,1},{1,0},{2,3},{3,2},{4,5},{5,4},{6,7},{7,6},{8,9},{9,8},{10,11... | collective-permute-start | bytes 49160 | tf_op jit(solution)/shard_map/ppermute | solution.py:527
  56.5 0.3 collective-permute-start.7
  56.8 1.4 %collective-permute-done.9 = f32[32,128]{1,0:T(8,128)S(1)} collective-permute-done((f32[32,128]{1,0:T(8,128)S(1)}, f32[32,128]{1,0:T(8,128)S(1)}, u32[]{:S(2)}, u32[]{:S(2)}) %collective-permute-start.9) | collective-permute-done | bytes 16416 | tf_op jit(solution)/shard_map/ppermute | solution.py:527
  58.2 0.5 collective-permute-done.8
  58.7 2.4 %collective-permute-done.7 = f32[32,128]{1,0:T(8,128)S(1)} collective-permute-done((f32[32,128]{1,0:T(8,128)S(1)}, f32[32,128]{1,0:T(8,128)S(1)}, u32[]{:S(2)}, u32[]{:S(2)}) %collective-permute-start.7) | collective-permute-done | bytes 16416 | tf_op jit(solution)/shard_map/ppermute | solution.py:527
  61.1 0.0 copy-done.1
  61.1 6.5 %modes.1 = (f32[2048,128]{1,0:T(8,128)}, f32[2048,128]{1,0:T(8,128)}) custom-call(s32[2,64]{1,0:T(2,128)S(1)} %pad_add_fusion.1.rank_ref, f32[32,128]{1,0:T(8,128)S(1)} %add_add_fusion.1.gram_ref, f32[32,64]{1,0:T(8,128)S(1)} %bitcast.18, bf16[32,128,256]{2,1,0:T(8,128)(2,1)S(1)} %get-tuple-element.20.direct_ref, ...), custom_call_target="tpu_custom_call" | custom-call | tf_op jit(solution)/shard_map/modes/pallas_call | solution.py:684
  (12 shorter events, 0.1 us)
Async XLA Ops:
  2.4 11.4 %collective-permute-start.1 = (f32[704,128]{1,0:T(8,128)}, f32[704,128]{1,0:T(8,128)S(1)}, u32[]{:S(2)}, u32[]{:S(2)}) collective-permute-start(f32[704,128]{1,0:T(8,128)} %stage.1.here), channel_id=1, source_target_pairs={{2,4},{4,2},{6,8},{8,6},{10,12},{12,10},{14,16},{16,14},{18,20},{2... | collective-permute-start | bytes 1081352 | tf_op jit(solution)/shard_map/ppermute | solution.py:580
  3.1 10.7 %collective-permute-start = (f32[704,128]{1,0:T(8,128)}, f32[704,128]{1,0:T(8,128)S(1)}, u32[]{:S(2)}, u32[]{:S(2)}) collective-permute-start(f32[704,128]{1,0:T(8,128)} %stage.1.here), channel_id=1, source_target_pairs={{0,2},{2,0},{4,6},{6,4},{8,10},{10,8},{12,14},{14,12},{16,18},{18,... | collective-permute-start | bytes 1081352 | tf_op jit(solution)/shard_map/ppermute | solution.py:579
  11.6 1.0 %copy-start = (f32[704,128]{1,0:T(8,128)S(1)}, f32[704,128]{1,0:T(8,128)}, u32[]{:S(2)}) copy-start(f32[704,128]{1,0:T(8,128)} %stage.1.here) | copy-start | bytes 1081348
  15.4 15.0 %collective-permute-start.2 = (f32[72,8,128]{2,1,0:T(8,128)S(1)}, f32[72,8,128]{2,1,0:T(8,128)S(1)}, u32[]{:S(2)}, u32[]{:S(2)}) collective-permute-start(f32[72,8,128]{2,1,0:T(8,128)S(1)} %get-tuple-element.14.rim_ref), channel_id=1, source_target_pairs={{0,1},{1,0},{2,3},{3,2},{4,5},{5,4},{6,7},{7,6},{8,9},{9,8},{10,11... | collective-permute-start | bytes 884744 | tf_op jit(solution)/shard_map/ppermute | solution.py:633
  30.4 30.7 %copy-start.1 = (f32[64,32]{0,1:T(8,128)S(1)}, f32[64,32]{0,1:T(8,128)}, u32[]{:S(2)}) copy-start(f32[64,32]{0,1:T(8,128)} %param.15) | copy-start | bytes 24580
  41.5 2.7 %collective-permute-start.3 = (f32[32,128]{1,0:T(8,128)S(1)}, f32[32,128]{1,0:T(8,128)S(1)}, u32[]{:S(2)}, u32[]{:S(2)}) collective-permute-start(f32[32,128]{1,0:T(8,128)S(1)} %get-tuple-element.19), channel_id=1, source_target_pairs={{0,2},{1,3},{2,0},{3,1},{4,6},{5,7},{6,4},{7,5},{8,10},{9,11},{10,... | collective-permute-start | bytes 49160 | tf_op jit(solution)/shard_map/ppermute | solution.py:527
  44.3 5.6 %collective-permute-start.6 = (f32[32,128]{1,0:T(8,128)S(1)}, f32[32,128]{1,0:T(8,128)S(1)}, u32[]{:S(2)}, u32[]{:S(2)}) collective-permute-start(f32[32,128]{1,0:T(8,128)S(1)} %add.30), channel_id=1, source_target_pairs={{0,12},{1,13},{2,14},{3,15},{4,8},{5,9},{6,10},{7,11},{8,4},{9,5},... | collective-permute-start | bytes 49160 | tf_op jit(solution)/shard_map/ppermute | solution.py:527
  48.2 3.7 %collective-permute-start.5 = (f32[32,128]{1,0:T(8,128)S(1)}, f32[32,128]{1,0:T(8,128)S(1)}, u32[]{:S(2)}, u32[]{:S(2)}) collective-permute-start(f32[32,128]{1,0:T(8,128)S(1)} %add.30), channel_id=1, source_target_pairs={{0,8},{1,9},{2,10},{3,11},{4,12},{5,13},{6,14},{7,15},{8,0},{9,1},... | collective-permute-start | bytes 49160 | tf_op jit(solution)/shard_map/ppermute | solution.py:527
  48.6 3.7 %collective-permute-start.4 = (f32[32,128]{1,0:T(8,128)S(1)}, f32[32,128]{1,0:T(8,128)S(1)}, u32[]{:S(2)}, u32[]{:S(2)}) collective-permute-start(f32[32,128]{1,0:T(8,128)S(1)} %add.30), channel_id=1, source_target_pairs={{0,4},{1,5},{2,6},{3,7},{4,0},{5,1},{6,2},{7,3},{8,12},{9,13},{10,... | collective-permute-start | bytes 49160 | tf_op jit(solution)/shard_map/ppermute | solution.py:527
  52.4 5.8 %collective-permute-start.9 = (f32[32,128]{1,0:T(8,128)S(1)}, f32[32,128]{1,0:T(8,128)S(1)}, u32[]{:S(2)}, u32[]{:S(2)}) collective-permute-start(f32[32,128]{1,0:T(8,128)S(1)} %add_add_fusion.2), channel_id=1, source_target_pairs={{0,17},{1,16},{2,19},{3,18},{4,21},{5,20},{6,23},{7,22},{8,25},{9,... | collective-permute-start | bytes 49160 | tf_op jit(solution)/shard_map/ppermute | solution.py:527
  55.0 3.7 %collective-permute-start.8 = (f32[32,128]{1,0:T(8,128)S(1)}, f32[32,128]{1,0:T(8,128)S(1)}, u32[]{:S(2)}, u32[]{:S(2)}) collective-permute-start(f32[32,128]{1,0:T(8,128)S(1)} %add_add_fusion.2), channel_id=1, source_target_pairs={{0,1},{1,0},{2,3},{3,2},{4,5},{5,4},{6,7},{7,6},{8,9},{9,8},{10,11... | collective-permute-start | bytes 49160 | tf_op jit(solution)/shard_map/ppermute | solution.py:527
  56.5 4.6 %collective-permute-start.7 = (f32[32,128]{1,0:T(8,128)S(1)}, f32[32,128]{1,0:T(8,128)S(1)}, u32[]{:S(2)}, u32[]{:S(2)}) collective-permute-start(f32[32,128]{1,0:T(8,128)S(1)} %add_add_fusion.2), channel_id=1, source_target_pairs={{0,16},{1,17},{2,18},{3,19},{4,20},{5,21},{6,22},{7,23},{8,24},{9,... | collective-permute-start | bytes 49160 | tf_op jit(solution)/shard_map/ppermute | solution.py:527
